TPU v7x, 32 devices: a whole 2x2x4 slice. The times are simulated.
32 devices in a mesh: seq: 16 (over z, y, core), batch: 2 (over x).
Axes of the slice: x: 2, y: 2, z: 4, core: 2. Of those that a mesh axis runs over, the one named last changes fastest.
Arguments:
- hidden_in: bfloat16 [2, 4096, 2304], P('batch', 'seq'), may hold values from -6 to 6
- segment_ids: int32 [2, 4096], P('batch', 'seq'), may hold values from 0 to 15, never falling along the last dimension, each value on 1 to 512 neighbouring positions
- pre_gain: float32 [2304], replicated, may hold values from 0.25 to 1.75
- w_qkv: bfloat16 [2304, 2048], P('seq'), may hold values from -0.27083333 to 0.27083333
- w_out: bfloat16 [1024, 2304], P('seq'), may hold values from -0.1875 to 0.1875
- post_gain: float32 [2304], replicated, may hold values from 0.25 to 1.75
Outputs:
- layer_out: bfloat16 [2, 4096, 2304], P('batch', 'seq')
Inputs may be any that keep to these rules, and one draw needn't show every extreme that they name: `segment_ids`: along each sequence the numbers never fall; a document is 1 to 512 positions long, and each sequence has one of exactly 512.
All inputs are finite; a program needn't handle non-finite values.
Results may differ from a plain program's by a relative error of at most 0.012.
The roundings to bfloat16 on the way count: a program that leaves them out, or rounds other values in their place, can miss the bound.
Values may be sent and summed in bfloat16 or wider, within the bound.
A program may use at most 128 MiB of HBM per device.

v0:
```python
import math

import jax
import jax.numpy as jnp
from jax import lax
from jax.sharding import PartitionSpec as P

Q_HEADS = 4
KV_HEADS = 2
HEAD = 256
WINDOW = 4096
DOCS = 16


EPS = 1e-06
CAP = 50.0


def from_behind(block, axis, distance):
    devices = range(lax.axis_size(axis))
    route = [(i - distance, i) for i in devices if i - distance in devices]
    return lax.ppermute(block, axis, route)


def rms_scale(values, gain):
    return values * lax.rsqrt(jnp.mean(values * values, axis=-1, keepdims=True) + EPS) * gain


def rotary(values, positions, leading):
    head_size = values.shape[-1]
    half_dim = head_size // 2
    inverse = 1.0 / 10000.0 ** (jnp.arange(half_dim, dtype=jnp.float32) * 2.0 / head_size)
    angles = positions.astype(jnp.float32)[:, None] * inverse[None, :]
    shape = (
        (1,) * leading + (positions.shape[0],) + (1,) * (values.ndim - 2 - leading) + (half_dim,)
    )
    cosine = jnp.cos(angles).reshape(shape)
    sine = jnp.sin(angles).reshape(shape)
    first_half = values[..., :half_dim]
    second_half = values[..., half_dim:]
    return jnp.concatenate(
        [first_half * cosine - second_half * sine, second_half * cosine + first_half * sine],
        axis=-1,
    )


def attend(states, queries, key_block, value_block, query_pos, key_pos, starts):
    running, totals = states
    scores = jnp.einsum(
        "qhgd,khd->qhgk", queries, key_block, preferred_element_type=jnp.float32
    ) * (1.0 / math.sqrt(HEAD))
    capped = CAP * jnp.tanh(scores / CAP)
    allowed = (
        (key_pos[None, :] <= query_pos[:, None])
        & (query_pos[:, None] - key_pos[None, :] < WINDOW)
        & (key_pos[None, :] >= starts[:, None])
    )
    weights = jnp.where(allowed[:, None, None, :], jnp.exp(capped), 0.0)
    totals = totals + jnp.sum(weights, axis=-1)
    running = running + jnp.einsum(
        "qhgk,khd->qhgd",
        weights.astype(jnp.bfloat16),
        value_block,
        preferred_element_type=jnp.float32,
    )
    return (running, totals)


def per_device(hidden_in, segment_ids, pre_gain, w_qkv, w_out, post_gain):
    tok_rows = hidden_in.shape[1]
    seq_count = lax.axis_size("seq")
    seq_index = lax.axis_index("seq")
    groups = Q_HEADS // KV_HEADS
    positions = seq_index * tok_rows + jnp.arange(tok_rows, dtype=jnp.int32)
    widened = hidden_in[0].astype(jnp.float32)
    normed = rms_scale(widened, pre_gain).astype(jnp.bfloat16)
    columns = normed
    projected = jnp.dot(
        columns,
        lax.all_gather(w_qkv, "seq", axis=0, tiled=True),
        preferred_element_type=jnp.float32,
    )
    queries = rotary(
        projected[:, : Q_HEADS * HEAD].reshape(tok_rows, KV_HEADS, groups, HEAD), positions, 0
    ).astype(jnp.bfloat16)
    key_rows = rotary(
        projected[:, Q_HEADS * HEAD : (Q_HEADS + KV_HEADS) * HEAD].reshape(
            tok_rows, KV_HEADS, HEAD
        ),
        positions,
        0,
    ).astype(jnp.bfloat16)
    value_rows = (
        projected[:, (Q_HEADS + KV_HEADS) * HEAD :]
        .reshape(tok_rows, KV_HEADS, HEAD)
        .astype(jnp.bfloat16)
    )
    doc_numbers = jnp.arange(DOCS, dtype=jnp.int32)
    matches = segment_ids[0][:, None] == doc_numbers[None, :]
    local_first = jnp.min(jnp.where(matches, positions[:, None], seq_count * tok_rows), axis=0)
    first_pos = lax.pmin(local_first, "seq")
    starts = jnp.sum(jnp.where(matches, first_pos[None, :], 0), axis=1)
    states = (
        jnp.zeros((tok_rows, KV_HEADS, groups, HEAD), jnp.float32),
        jnp.zeros((tok_rows, KV_HEADS, groups), jnp.float32),
    )
    states = attend(states, queries, key_rows, value_rows, positions, positions, starts)
    hop_count = min(WINDOW // tok_rows, seq_count - 1)

    def relay_step(hop_index, carried):
        moving_keys, moving_values, running, totals = carried
        moving_keys, moving_values = from_behind((moving_keys, moving_values), "seq", 1)
        running, totals = attend(
            (running, totals),
            queries,
            moving_keys,
            moving_values,
            positions,
            positions - hop_index * tok_rows,
            starts,
        )
        return (moving_keys, moving_values, running, totals)

    carried = lax.fori_loop(
        1, hop_count + 1, relay_step, (key_rows, value_rows, states[0], states[1])
    )
    states = (carried[2], carried[3])
    running, totals = states
    attended = (running / totals[..., None]).astype(jnp.bfloat16).reshape(tok_rows, Q_HEADS * HEAD)
    columns = attended
    branch = jnp.dot(
        columns,
        lax.all_gather(w_out, "seq", axis=0, tiled=True),
        preferred_element_type=jnp.float32,
    )
    return (widened + rms_scale(branch, post_gain)).astype(jnp.bfloat16)[None]


def solution(mesh):
    placed = (P("batch", "seq", None), P("batch", "seq"), P(), P("seq", None), P("seq", None), P())
    return jax.shard_map(
        per_device, mesh=mesh, in_specs=placed, out_specs=P("batch", "seq", None), check_vma=False
    )
```

profile of v0, /device:TPU:1, one launch (start us, length us, event | category | flops | bytes accessed | tf_op | source)
XLA Modules:
  0.0 309.2 jit_solution(5718525770423550669)
XLA Ops:
  10.4 10.7 %pmin.7 = s32[16]{0:T(128)S(1)} all-reduce(s32[16]{0:T(128)S(1)} %select_reduce_fusion.1), channel_id=1, replica_groups=mesh['seq'=16,'batch'=2] {'seq'}, use_global_device_ids=true, to_apply=%region_2.3 | all-reduce | flops 16 | bytes 128 | tf_op jit(solution)/shard_map/pmin | solution.py:101
  23.9 69.1 %all-gather.3.cloned.1.call-done = bf16[2304,2048]{1,0:T(8,128)(2,1)} async-done(((bf16[144,2048]{1,0:T(8,128)(2,1)}), bf16[2304,2048]{1,0:T(8,128)(2,1)}) %all-gather.3.cloned.1.call-update) | async-done | bytes 9437200 | tf_op jit(solution)/shard_map/all_gather | solution.py:80
  93.0 5.2 %fusion.23 = f32[256,2048]{1,0:T(8,128)S(1)} fusion(bf16[2304,2048]{1,0:T(8,128)(2,1)} %all-gather.3.cloned.1.call-done, bf16[1,256,2304]{2,1,0:T(8,128)(2,1)S(1)} %copy-done, f32[2304]{0:T(1024)S(1)} %copy-done.7, f32[256]{0:T(256)S(1)} %add_rsqrt_fusion.1), kind=kOutput, calls=%fused_computation.33 | convolution fusion | flops 2418278400 | bytes 12724224 | tf_op jit(solution)/shard_map/dot_general | solution.py:78
  106.9 189.7 %while.22 = (s32[]{:T(128)}, bf16[256,2,256]{2,0,1:T(8,128)(2,1)}, bf16[256,2,256]{2,0,1:T(8,128)(2,1)S(1)}, f32[256,2,2,256]{3,0,2,1:T(8,128)S(1)}, f32[256,2,2...) while((s32[]{:T(128)}, bf16[256,2,256]{2,0,1:T(8,128)(2,1)}, ...), condition=%wide.region_7.8_spmd.clone, body=%wide.region_5.7_spmd.clone.sunk | while | flops 270402048 | bytes 7492809 | solution.py:124
  116.1 4.4 %collective-permute-start = (bf16[256,2,256]{2,0,1:T(8,128)(2,1)}, bf16[256,2,256]{2,0,1:T(8,128)(2,1)S(1)}, u32[]{:S(2)}, u32[]{:S(2)}) collective-permute-start(bf16[256,2,256]{2,0,1:T(8,128)(2,1)} %get-tuple-element.355), channel_id=1, source_target_pairs={{0,2},{2,4},{4,6},{6,8},{8,10},{10,12},{12,14},{14,16},{16,18},{18... | collective-permute-start | bytes 786440 | tf_op jit(solution)/shard_map/while/body/eval_jaxpr/ppermute | solution.py:22
  120.5 3.9 %collective-permute-start.1 = (bf16[256,2,256]{2,0,1:T(8,128)(2,1)S(1)}, bf16[256,2,256]{2,0,1:T(8,128)(2,1)S(1)}, u32[]{:S(2)}, u32[]{:S(2)}) collective-permute-start(bf16[256,2,256]{2,0,1:T(8,128)(2,1)S(1)} %get-tuple-element.356), channel_id=1, source_target_pairs={{0,2},{2,4},{4,6},{6,8},{8,10},{10,12},{12,14},{14,16},{16,18},{18... | collective-permute-start | bytes 786440 | tf_op jit(solution)/shard_map/while/body/eval_jaxpr/ppermute | solution.py:22
  124.6 4.8 %collective-permute-done = bf16[256,2,256]{2,0,1:T(8,128)(2,1)S(1)} collective-permute-done((bf16[256,2,256]{2,0,1:T(8,128)(2,1)}, bf16[256,2,256]{2,0,1:T(8,128)(2,1)S(1)}, u32[]{:S(2)}, u32[]{:S(2)}) %collective-permute-start) | collective-permute-done | bytes 262176 | tf_op jit(solution)/shard_map/while/body/eval_jaxpr/ppermute | solution.py:22
  131.7 6.0 %collective-permute-done.1 = bf16[256,2,256]{2,0,1:T(8,128)(2,1)S(1)} collective-permute-done((bf16[256,2,256]{2,0,1:T(8,128)(2,1)S(1)}, bf16[256,2,256]{2,0,1:T(8,128)(2,1)S(1)}, u32[]{:S(2)}, u32[]{:S(2)}) %collective-permute-start.1) | collective-permute-done | bytes 262176 | tf_op jit(solution)/shard_map/while/body/eval_jaxpr/ppermute | solution.py:22
  138.2 4.4 %collective-permute-start = (bf16[256,2,256]{2,0,1:T(8,128)(2,1)}, bf16[256,2,256]{2,0,1:T(8,128)(2,1)S(1)}, u32[]{:S(2)}, u32[]{:S(2)}) collective-permute-start(bf16[256,2,256]{2,0,1:T(8,128)(2,1)} %get-tuple-element.355), channel_id=1, source_target_pairs={{0,2},{2,4},{4,6},{6,8},{8,10},{10,12},{12,14},{14,16},{16,18},{18... | collective-permute-start | bytes 786440 | tf_op jit(solution)/shard_map/while/body/eval_jaxpr/ppermute | solution.py:22
  149.5 4.4 %collective-permute-start = (bf16[256,2,256]{2,0,1:T(8,128)(2,1)}, bf16[256,2,256]{2,0,1:T(8,128)(2,1)S(1)}, u32[]{:S(2)}, u32[]{:S(2)}) collective-permute-start(bf16[256,2,256]{2,0,1:T(8,128)(2,1)} %get-tuple-element.355), channel_id=1, source_target_pairs={{0,2},{2,4},{4,6},{6,8},{8,10},{10,12},{12,14},{14,16},{16,18},{18... | collective-permute-start | bytes 786440 | tf_op jit(solution)/shard_map/while/body/eval_jaxpr/ppermute | solution.py:22
  153.9 5.3 %collective-permute-start.1 = (bf16[256,2,256]{2,0,1:T(8,128)(2,1)S(1)}, bf16[256,2,256]{2,0,1:T(8,128)(2,1)S(1)}, u32[]{:S(2)}, u32[]{:S(2)}) collective-permute-start(bf16[256,2,256]{2,0,1:T(8,128)(2,1)S(1)} %get-tuple-element.356), channel_id=1, source_target_pairs={{0,2},{2,4},{4,6},{6,8},{8,10},{10,12},{12,14},{14,16},{16,18},{18... | collective-permute-start | bytes 786440 | tf_op jit(solution)/shard_map/while/body/eval_jaxpr/ppermute | solution.py:22
  163.0 4.5 %collective-permute-start = (bf16[256,2,256]{2,0,1:T(8,128)(2,1)}, bf16[256,2,256]{2,0,1:T(8,128)(2,1)S(1)}, u32[]{:S(2)}, u32[]{:S(2)}) collective-permute-start(bf16[256,2,256]{2,0,1:T(8,128)(2,1)} %get-tuple-element.355), channel_id=1, source_target_pairs={{0,2},{2,4},{4,6},{6,8},{8,10},{10,12},{12,14},{14,16},{16,18},{18... | collective-permute-start | bytes 786440 | tf_op jit(solution)/shard_map/while/body/eval_jaxpr/ppermute | solution.py:22
  175.1 4.5 %collective-permute-start = (bf16[256,2,256]{2,0,1:T(8,128)(2,1)}, bf16[256,2,256]{2,0,1:T(8,128)(2,1)S(1)}, u32[]{:S(2)}, u32[]{:S(2)}) collective-permute-start(bf16[256,2,256]{2,0,1:T(8,128)(2,1)} %get-tuple-element.355), channel_id=1, source_target_pairs={{0,2},{2,4},{4,6},{6,8},{8,10},{10,12},{12,14},{14,16},{16,18},{18... | collective-permute-start | bytes 786440 | tf_op jit(solution)/shard_map/while/body/eval_jaxpr/ppermute | solution.py:22
  187.3 4.5 %collective-permute-start = (bf16[256,2,256]{2,0,1:T(8,128)(2,1)}, bf16[256,2,256]{2,0,1:T(8,128)(2,1)S(1)}, u32[]{:S(2)}, u32[]{:S(2)}) collective-permute-start(bf16[256,2,256]{2,0,1:T(8,128)(2,1)} %get-tuple-element.355), channel_id=1, source_target_pairs={{0,2},{2,4},{4,6},{6,8},{8,10},{10,12},{12,14},{14,16},{16,18},{18... | collective-permute-start | bytes 786440 | tf_op jit(solution)/shard_map/while/body/eval_jaxpr/ppermute | solution.py:22
  191.7 3.8 %collective-permute-start.1 = (bf16[256,2,256]{2,0,1:T(8,128)(2,1)S(1)}, bf16[256,2,256]{2,0,1:T(8,128)(2,1)S(1)}, u32[]{:S(2)}, u32[]{:S(2)}) collective-permute-start(bf16[256,2,256]{2,0,1:T(8,128)(2,1)S(1)} %get-tuple-element.356), channel_id=1, source_target_pairs={{0,2},{2,4},{4,6},{6,8},{8,10},{10,12},{12,14},{14,16},{16,18},{18... | collective-permute-start | bytes 786440 | tf_op jit(solution)/shard_map/while/body/eval_jaxpr/ppermute | solution.py:22
  199.4 4.5 %collective-permute-start = (bf16[256,2,256]{2,0,1:T(8,128)(2,1)}, bf16[256,2,256]{2,0,1:T(8,128)(2,1)S(1)}, u32[]{:S(2)}, u32[]{:S(2)}) collective-permute-start(bf16[256,2,256]{2,0,1:T(8,128)(2,1)} %get-tuple-element.355), channel_id=1, source_target_pairs={{0,2},{2,4},{4,6},{6,8},{8,10},{10,12},{12,14},{14,16},{16,18},{18... | collective-permute-start | bytes 786440 | tf_op jit(solution)/shard_map/while/body/eval_jaxpr/ppermute | solution.py:22
  203.9 3.8 %collective-permute-start.1 = (bf16[256,2,256]{2,0,1:T(8,128)(2,1)S(1)}, bf16[256,2,256]{2,0,1:T(8,128)(2,1)S(1)}, u32[]{:S(2)}, u32[]{:S(2)}) collective-permute-start(bf16[256,2,256]{2,0,1:T(8,128)(2,1)S(1)} %get-tuple-element.356), channel_id=1, source_target_pairs={{0,2},{2,4},{4,6},{6,8},{8,10},{10,12},{12,14},{14,16},{16,18},{18... | collective-permute-start | bytes 786440 | tf_op jit(solution)/shard_map/while/body/eval_jaxpr/ppermute | solution.py:22
  211.6 4.5 %collective-permute-start = (bf16[256,2,256]{2,0,1:T(8,128)(2,1)}, bf16[256,2,256]{2,0,1:T(8,128)(2,1)S(1)}, u32[]{:S(2)}, u32[]{:S(2)}) collective-permute-start(bf16[256,2,256]{2,0,1:T(8,128)(2,1)} %get-tuple-element.355), channel_id=1, source_target_pairs={{0,2},{2,4},{4,6},{6,8},{8,10},{10,12},{12,14},{14,16},{16,18},{18... | collective-permute-start | bytes 786440 | tf_op jit(solution)/shard_map/while/body/eval_jaxpr/ppermute | solution.py:22
  216.0 3.8 %collective-permute-start.1 = (bf16[256,2,256]{2,0,1:T(8,128)(2,1)S(1)}, bf16[256,2,256]{2,0,1:T(8,128)(2,1)S(1)}, u32[]{:S(2)}, u32[]{:S(2)}) collective-permute-start(bf16[256,2,256]{2,0,1:T(8,128)(2,1)S(1)} %get-tuple-element.356), channel_id=1, source_target_pairs={{0,2},{2,4},{4,6},{6,8},{8,10},{10,12},{12,14},{14,16},{16,18},{18... | collective-permute-start | bytes 786440 | tf_op jit(solution)/shard_map/while/body/eval_jaxpr/ppermute | solution.py:22
  223.7 4.5 %collective-permute-start = (bf16[256,2,256]{2,0,1:T(8,128)(2,1)}, bf16[256,2,256]{2,0,1:T(8,128)(2,1)S(1)}, u32[]{:S(2)}, u32[]{:S(2)}) collective-permute-start(bf16[256,2,256]{2,0,1:T(8,128)(2,1)} %get-tuple-element.355), channel_id=1, source_target_pairs={{0,2},{2,4},{4,6},{6,8},{8,10},{10,12},{12,14},{14,16},{16,18},{18... | collective-permute-start | bytes 786440 | tf_op jit(solution)/shard_map/while/body/eval_jaxpr/ppermute | solution.py:22
  228.2 3.8 %collective-permute-start.1 = (bf16[256,2,256]{2,0,1:T(8,128)(2,1)S(1)}, bf16[256,2,256]{2,0,1:T(8,128)(2,1)S(1)}, u32[]{:S(2)}, u32[]{:S(2)}) collective-permute-start(bf16[256,2,256]{2,0,1:T(8,128)(2,1)S(1)} %get-tuple-element.356), channel_id=1, source_target_pairs={{0,2},{2,4},{4,6},{6,8},{8,10},{10,12},{12,14},{14,16},{16,18},{18... | collective-permute-start | bytes 786440 | tf_op jit(solution)/shard_map/while/body/eval_jaxpr/ppermute | solution.py:22
  235.8 4.5 %collective-permute-start = (bf16[256,2,256]{2,0,1:T(8,128)(2,1)}, bf16[256,2,256]{2,0,1:T(8,128)(2,1)S(1)}, u32[]{:S(2)}, u32[]{:S(2)}) collective-permute-start(bf16[256,2,256]{2,0,1:T(8,128)(2,1)} %get-tuple-element.355), channel_id=1, source_target_pairs={{0,2},{2,4},{4,6},{6,8},{8,10},{10,12},{12,14},{14,16},{16,18},{18... | collective-permute-start | bytes 786440 | tf_op jit(solution)/shard_map/while/body/eval_jaxpr/ppermute | solution.py:22
  240.3 3.8 %collective-permute-start.1 = (bf16[256,2,256]{2,0,1:T(8,128)(2,1)S(1)}, bf16[256,2,256]{2,0,1:T(8,128)(2,1)S(1)}, u32[]{:S(2)}, u32[]{:S(2)}) collective-permute-start(bf16[256,2,256]{2,0,1:T(8,128)(2,1)S(1)} %get-tuple-element.356), channel_id=1, source_target_pairs={{0,2},{2,4},{4,6},{6,8},{8,10},{10,12},{12,14},{14,16},{16,18},{18... | collective-permute-start | bytes 786440 | tf_op jit(solution)/shard_map/while/body/eval_jaxpr/ppermute | solution.py:22
  248.0 4.5 %collective-permute-start = (bf16[256,2,256]{2,0,1:T(8,128)(2,1)}, bf16[256,2,256]{2,0,1:T(8,128)(2,1)S(1)}, u32[]{:S(2)}, u32[]{:S(2)}) collective-permute-start(bf16[256,2,256]{2,0,1:T(8,128)(2,1)} %get-tuple-element.355), channel_id=1, source_target_pairs={{0,2},{2,4},{4,6},{6,8},{8,10},{10,12},{12,14},{14,16},{16,18},{18... | collective-permute-start | bytes 786440 | tf_op jit(solution)/shard_map/while/body/eval_jaxpr/ppermute | solution.py:22
  252.5 3.8 %collective-permute-start.1 = (bf16[256,2,256]{2,0,1:T(8,128)(2,1)S(1)}, bf16[256,2,256]{2,0,1:T(8,128)(2,1)S(1)}, u32[]{:S(2)}, u32[]{:S(2)}) collective-permute-start(bf16[256,2,256]{2,0,1:T(8,128)(2,1)S(1)} %get-tuple-element.356), channel_id=1, source_target_pairs={{0,2},{2,4},{4,6},{6,8},{8,10},{10,12},{12,14},{14,16},{16,18},{18... | collective-permute-start | bytes 786440 | tf_op jit(solution)/shard_map/while/body/eval_jaxpr/ppermute | solution.py:22
  260.1 4.5 %collective-permute-start = (bf16[256,2,256]{2,0,1:T(8,128)(2,1)}, bf16[256,2,256]{2,0,1:T(8,128)(2,1)S(1)}, u32[]{:S(2)}, u32[]{:S(2)}) collective-permute-start(bf16[256,2,256]{2,0,1:T(8,128)(2,1)} %get-tuple-element.355), channel_id=1, source_target_pairs={{0,2},{2,4},{4,6},{6,8},{8,10},{10,12},{12,14},{14,16},{16,18},{18... | collective-permute-start | bytes 786440 | tf_op jit(solution)/shard_map/while/body/eval_jaxpr/ppermute | solution.py:22
  264.6 3.8 %collective-permute-start.1 = (bf16[256,2,256]{2,0,1:T(8,128)(2,1)S(1)}, bf16[256,2,256]{2,0,1:T(8,128)(2,1)S(1)}, u32[]{:S(2)}, u32[]{:S(2)}) collective-permute-start(bf16[256,2,256]{2,0,1:T(8,128)(2,1)S(1)} %get-tuple-element.356), channel_id=1, source_target_pairs={{0,2},{2,4},{4,6},{6,8},{8,10},{10,12},{12,14},{14,16},{16,18},{18... | collective-permute-start | bytes 786440 | tf_op jit(solution)/shard_map/while/body/eval_jaxpr/ppermute | solution.py:22
  272.3 4.5 %collective-permute-start = (bf16[256,2,256]{2,0,1:T(8,128)(2,1)}, bf16[256,2,256]{2,0,1:T(8,128)(2,1)S(1)}, u32[]{:S(2)}, u32[]{:S(2)}) collective-permute-start(bf16[256,2,256]{2,0,1:T(8,128)(2,1)} %get-tuple-element.355), channel_id=1, source_target_pairs={{0,2},{2,4},{4,6},{6,8},{8,10},{10,12},{12,14},{14,16},{16,18},{18... | collective-permute-start | bytes 786440 | tf_op jit(solution)/shard_map/while/body/eval_jaxpr/ppermute | solution.py:22
  276.7 3.8 %collective-permute-start.1 = (bf16[256,2,256]{2,0,1:T(8,128)(2,1)S(1)}, bf16[256,2,256]{2,0,1:T(8,128)(2,1)S(1)}, u32[]{:S(2)}, u32[]{:S(2)}) collective-permute-start(bf16[256,2,256]{2,0,1:T(8,128)(2,1)S(1)} %get-tuple-element.356), channel_id=1, source_target_pairs={{0,2},{2,4},{4,6},{6,8},{8,10},{10,12},{12,14},{14,16},{16,18},{18... | collective-permute-start | bytes 786440 | tf_op jit(solution)/shard_map/while/body/eval_jaxpr/ppermute | solution.py:22
  284.4 4.5 %collective-permute-start = (bf16[256,2,256]{2,0,1:T(8,128)(2,1)}, bf16[256,2,256]{2,0,1:T(8,128)(2,1)S(1)}, u32[]{:S(2)}, u32[]{:S(2)}) collective-permute-start(bf16[256,2,256]{2,0,1:T(8,128)(2,1)} %get-tuple-element.355), channel_id=1, source_target_pairs={{0,2},{2,4},{4,6},{6,8},{8,10},{10,12},{12,14},{14,16},{16,18},{18... | collective-permute-start | bytes 786440 | tf_op jit(solution)/shard_map/while/body/eval_jaxpr/ppermute | solution.py:22
  288.9 3.8 %collective-permute-start.1 = (bf16[256,2,256]{2,0,1:T(8,128)(2,1)S(1)}, bf16[256,2,256]{2,0,1:T(8,128)(2,1)S(1)}, u32[]{:S(2)}, u32[]{:S(2)}) collective-permute-start(bf16[256,2,256]{2,0,1:T(8,128)(2,1)S(1)} %get-tuple-element.356), channel_id=1, source_target_pairs={{0,2},{2,4},{4,6},{6,8},{8,10},{10,12},{12,14},{14,16},{16,18},{18... | collective-permute-start | bytes 786440 | tf_op jit(solution)/shard_map/while/body/eval_jaxpr/ppermute | solution.py:22
  297.0 3.9 %multiply_reduce_fusion = (f32[256]{0:T(256)S(1)}, f32[256,2304]{1,0:T(8,128)S(1)}) fusion(bf16[256,1024]{0,1:T(8,128)(2,1)S(1)} %bitcast.66, bf16[1024,2304]{1,0:T(8,128)(2,1)} %all-gather.5.cloned.1.call-done), kind=kOutput, calls=%fused_computation.24 | convolution fusion | flops 1209138944 | bytes 7603200 | tf_op jit(solution)/shard_map/dot_general | solution.py:131
  (188 shorter events, 88.7 us)
Async XLA Ops:
  6.5 86.5 %all-gather.3.cloned.1.call-start = ((), (), s32[]{:S(2)}) async-start(), calls=%async_computation | async-start | bytes 10027008 | tf_op jit(solution)/shard_map/all_gather | solution.py:80
  7.3 289.8 %all-gather.5.cloned.1.call-start = ((), (), s32[]{:S(2)}) async-start(), calls=%async_computation.1 | async-start | bytes 5013504 | tf_op jit(solution)/shard_map/all_gather | solution.py:133
  106.9 6.0 %collective-permute-start = (bf16[256,2,256]{2,0,1:T(8,128)(2,1)}, bf16[256,2,256]{2,0,1:T(8,128)(2,1)S(1)}, u32[]{:S(2)}, u32[]{:S(2)}) collective-permute-start(bf16[256,2,256]{2,0,1:T(8,128)(2,1)} %get-tuple-element.355), channel_id=1, source_target_pairs={{0,2},{2,4},{4,6},{6,8},{8,10},{10,12},{12,14},{14,16},{16,18},{18... | collective-permute-start | bytes 786440 | tf_op jit(solution)/shard_map/while/body/eval_jaxpr/ppermute | solution.py:22
  109.3 6.3 %collective-permute-start.1 = (bf16[256,2,256]{2,0,1:T(8,128)(2,1)S(1)}, bf16[256,2,256]{2,0,1:T(8,128)(2,1)S(1)}, u32[]{:S(2)}, u32[]{:S(2)}) collective-permute-start(bf16[256,2,256]{2,0,1:T(8,128)(2,1)S(1)} %get-tuple-element.356), channel_id=1, source_target_pairs={{0,2},{2,4},{4,6},{6,8},{8,10},{10,12},{12,14},{14,16},{16,18},{18... | collective-permute-start | bytes 786440 | tf_op jit(solution)/shard_map/while/body/eval_jaxpr/ppermute | solution.py:22
  116.1 13.3 %collective-permute-start = (bf16[256,2,256]{2,0,1:T(8,128)(2,1)}, bf16[256,2,256]{2,0,1:T(8,128)(2,1)S(1)}, u32[]{:S(2)}, u32[]{:S(2)}) collective-permute-start(bf16[256,2,256]{2,0,1:T(8,128)(2,1)} %get-tuple-element.355), channel_id=1, source_target_pairs={{0,2},{2,4},{4,6},{6,8},{8,10},{10,12},{12,14},{14,16},{16,18},{18... | collective-permute-start | bytes 786440 | tf_op jit(solution)/shard_map/while/body/eval_jaxpr/ppermute | solution.py:22
  120.5 17.2 %collective-permute-start.1 = (bf16[256,2,256]{2,0,1:T(8,128)(2,1)S(1)}, bf16[256,2,256]{2,0,1:T(8,128)(2,1)S(1)}, u32[]{:S(2)}, u32[]{:S(2)}) collective-permute-start(bf16[256,2,256]{2,0,1:T(8,128)(2,1)S(1)} %get-tuple-element.356), channel_id=1, source_target_pairs={{0,2},{2,4},{4,6},{6,8},{8,10},{10,12},{12,14},{14,16},{16,18},{18... | collective-permute-start | bytes 786440 | tf_op jit(solution)/shard_map/while/body/eval_jaxpr/ppermute | solution.py:22
  138.2 8.0 %collective-permute-start = (bf16[256,2,256]{2,0,1:T(8,128)(2,1)}, bf16[256,2,256]{2,0,1:T(8,128)(2,1)S(1)}, u32[]{:S(2)}, u32[]{:S(2)}) collective-permute-start(bf16[256,2,256]{2,0,1:T(8,128)(2,1)} %get-tuple-element.355), channel_id=1, source_target_pairs={{0,2},{2,4},{4,6},{6,8},{8,10},{10,12},{12,14},{14,16},{16,18},{18... | collective-permute-start | bytes 786440 | tf_op jit(solution)/shard_map/while/body/eval_jaxpr/ppermute | solution.py:22
  142.6 6.3 %collective-permute-start.1 = (bf16[256,2,256]{2,0,1:T(8,128)(2,1)S(1)}, bf16[256,2,256]{2,0,1:T(8,128)(2,1)S(1)}, u32[]{:S(2)}, u32[]{:S(2)}) collective-permute-start(bf16[256,2,256]{2,0,1:T(8,128)(2,1)S(1)} %get-tuple-element.356), channel_id=1, source_target_pairs={{0,2},{2,4},{4,6},{6,8},{8,10},{10,12},{12,14},{14,16},{16,18},{18... | collective-permute-start | bytes 786440 | tf_op jit(solution)/shard_map/while/body/eval_jaxpr/ppermute | solution.py:22
  149.5 9.8 %collective-permute-start = (bf16[256,2,256]{2,0,1:T(8,128)(2,1)}, bf16[256,2,256]{2,0,1:T(8,128)(2,1)S(1)}, u32[]{:S(2)}, u32[]{:S(2)}) collective-permute-start(bf16[256,2,256]{2,0,1:T(8,128)(2,1)} %get-tuple-element.355), channel_id=1, source_target_pairs={{0,2},{2,4},{4,6},{6,8},{8,10},{10,12},{12,14},{14,16},{16,18},{18... | collective-permute-start | bytes 786440 | tf_op jit(solution)/shard_map/while/body/eval_jaxpr/ppermute | solution.py:22
  153.9 8.6 %collective-permute-start.1 = (bf16[256,2,256]{2,0,1:T(8,128)(2,1)S(1)}, bf16[256,2,256]{2,0,1:T(8,128)(2,1)S(1)}, u32[]{:S(2)}, u32[]{:S(2)}) collective-permute-start(bf16[256,2,256]{2,0,1:T(8,128)(2,1)S(1)} %get-tuple-element.356), channel_id=1, source_target_pairs={{0,2},{2,4},{4,6},{6,8},{8,10},{10,12},{12,14},{14,16},{16,18},{18... | collective-permute-start | bytes 786440 | tf_op jit(solution)/shard_map/while/body/eval_jaxpr/ppermute | solution.py:22
  163.0 8.5 %collective-permute-start = (bf16[256,2,256]{2,0,1:T(8,128)(2,1)}, bf16[256,2,256]{2,0,1:T(8,128)(2,1)S(1)}, u32[]{:S(2)}, u32[]{:S(2)}) collective-permute-start(bf16[256,2,256]{2,0,1:T(8,128)(2,1)} %get-tuple-element.355), channel_id=1, source_target_pairs={{0,2},{2,4},{4,6},{6,8},{8,10},{10,12},{12,14},{14,16},{16,18},{18... | collective-permute-start | bytes 786440 | tf_op jit(solution)/shard_map/while/body/eval_jaxpr/ppermute | solution.py:22
  167.5 7.1 %collective-permute-start.1 = (bf16[256,2,256]{2,0,1:T(8,128)(2,1)S(1)}, bf16[256,2,256]{2,0,1:T(8,128)(2,1)S(1)}, u32[]{:S(2)}, u32[]{:S(2)}) collective-permute-start(bf16[256,2,256]{2,0,1:T(8,128)(2,1)S(1)} %get-tuple-element.356), channel_id=1, source_target_pairs={{0,2},{2,4},{4,6},{6,8},{8,10},{10,12},{12,14},{14,16},{16,18},{18... | collective-permute-start | bytes 786440 | tf_op jit(solution)/shard_map/while/body/eval_jaxpr/ppermute | solution.py:22
  175.1 8.5 %collective-permute-start = (bf16[256,2,256]{2,0,1:T(8,128)(2,1)}, bf16[256,2,256]{2,0,1:T(8,128)(2,1)S(1)}, u32[]{:S(2)}, u32[]{:S(2)}) collective-permute-start(bf16[256,2,256]{2,0,1:T(8,128)(2,1)} %get-tuple-element.355), channel_id=1, source_target_pairs={{0,2},{2,4},{4,6},{6,8},{8,10},{10,12},{12,14},{14,16},{16,18},{18... | collective-permute-start | bytes 786440 | tf_op jit(solution)/shard_map/while/body/eval_jaxpr/ppermute | solution.py:22
  179.6 7.1 %collective-permute-start.1 = (bf16[256,2,256]{2,0,1:T(8,128)(2,1)S(1)}, bf16[256,2,256]{2,0,1:T(8,128)(2,1)S(1)}, u32[]{:S(2)}, u32[]{:S(2)}) collective-permute-start(bf16[256,2,256]{2,0,1:T(8,128)(2,1)S(1)} %get-tuple-element.356), channel_id=1, source_target_pairs={{0,2},{2,4},{4,6},{6,8},{8,10},{10,12},{12,14},{14,16},{16,18},{18... | collective-permute-start | bytes 786440 | tf_op jit(solution)/shard_map/while/body/eval_jaxpr/ppermute | solution.py:22
  187.3 8.5 %collective-permute-start = (bf16[256,2,256]{2,0,1:T(8,128)(2,1)}, bf16[256,2,256]{2,0,1:T(8,128)(2,1)S(1)}, u32[]{:S(2)}, u32[]{:S(2)}) collective-permute-start(bf16[256,2,256]{2,0,1:T(8,128)(2,1)} %get-tuple-element.355), channel_id=1, source_target_pairs={{0,2},{2,4},{4,6},{6,8},{8,10},{10,12},{12,14},{14,16},{16,18},{18... | collective-permute-start | bytes 786440 | tf_op jit(solution)/shard_map/while/body/eval_jaxpr/ppermute | solution.py:22
  191.7 7.1 %collective-permute-start.1 = (bf16[256,2,256]{2,0,1:T(8,128)(2,1)S(1)}, bf16[256,2,256]{2,0,1:T(8,128)(2,1)S(1)}, u32[]{:S(2)}, u32[]{:S(2)}) collective-permute-start(bf16[256,2,256]{2,0,1:T(8,128)(2,1)S(1)} %get-tuple-element.356), channel_id=1, source_target_pairs={{0,2},{2,4},{4,6},{6,8},{8,10},{10,12},{12,14},{14,16},{16,18},{18... | collective-permute-start | bytes 786440 | tf_op jit(solution)/shard_map/while/body/eval_jaxpr/ppermute | solution.py:22
  199.4 8.5 %collective-permute-start = (bf16[256,2,256]{2,0,1:T(8,128)(2,1)}, bf16[256,2,256]{2,0,1:T(8,128)(2,1)S(1)}, u32[]{:S(2)}, u32[]{:S(2)}) collective-permute-start(bf16[256,2,256]{2,0,1:T(8,128)(2,1)} %get-tuple-element.355), channel_id=1, source_target_pairs={{0,2},{2,4},{4,6},{6,8},{8,10},{10,12},{12,14},{14,16},{16,18},{18... | collective-permute-start | bytes 786440 | tf_op jit(solution)/shard_map/while/body/eval_jaxpr/ppermute | solution.py:22
  203.9 7.1 %collective-permute-start.1 = (bf16[256,2,256]{2,0,1:T(8,128)(2,1)S(1)}, bf16[256,2,256]{2,0,1:T(8,128)(2,1)S(1)}, u32[]{:S(2)}, u32[]{:S(2)}) collective-permute-start(bf16[256,2,256]{2,0,1:T(8,128)(2,1)S(1)} %get-tuple-element.356), channel_id=1, source_target_pairs={{0,2},{2,4},{4,6},{6,8},{8,10},{10,12},{12,14},{14,16},{16,18},{18... | collective-permute-start | bytes 786440 | tf_op jit(solution)/shard_map/while/body/eval_jaxpr/ppermute | solution.py:22
  211.6 8.5 %collective-permute-start = (bf16[256,2,256]{2,0,1:T(8,128)(2,1)}, bf16[256,2,256]{2,0,1:T(8,128)(2,1)S(1)}, u32[]{:S(2)}, u32[]{:S(2)}) collective-permute-start(bf16[256,2,256]{2,0,1:T(8,128)(2,1)} %get-tuple-element.355), channel_id=1, source_target_pairs={{0,2},{2,4},{4,6},{6,8},{8,10},{10,12},{12,14},{14,16},{16,18},{18... | collective-permute-start | bytes 786440 | tf_op jit(solution)/shard_map/while/body/eval_jaxpr/ppermute | solution.py:22
  216.0 7.1 %collective-permute-start.1 = (bf16[256,2,256]{2,0,1:T(8,128)(2,1)S(1)}, bf16[256,2,256]{2,0,1:T(8,128)(2,1)S(1)}, u32[]{:S(2)}, u32[]{:S(2)}) collective-permute-start(bf16[256,2,256]{2,0,1:T(8,128)(2,1)S(1)} %get-tuple-element.356), channel_id=1, source_target_pairs={{0,2},{2,4},{4,6},{6,8},{8,10},{10,12},{12,14},{14,16},{16,18},{18... | collective-permute-start | bytes 786440 | tf_op jit(solution)/shard_map/while/body/eval_jaxpr/ppermute | solution.py:22
  223.7 8.5 %collective-permute-start = (bf16[256,2,256]{2,0,1:T(8,128)(2,1)}, bf16[256,2,256]{2,0,1:T(8,128)(2,1)S(1)}, u32[]{:S(2)}, u32[]{:S(2)}) collective-permute-start(bf16[256,2,256]{2,0,1:T(8,128)(2,1)} %get-tuple-element.355), channel_id=1, source_target_pairs={{0,2},{2,4},{4,6},{6,8},{8,10},{10,12},{12,14},{14,16},{16,18},{18... | collective-permute-start | bytes 786440 | tf_op jit(solution)/shard_map/while/body/eval_jaxpr/ppermute | solution.py:22
  228.2 7.1 %collective-permute-start.1 = (bf16[256,2,256]{2,0,1:T(8,128)(2,1)S(1)}, bf16[256,2,256]{2,0,1:T(8,128)(2,1)S(1)}, u32[]{:S(2)}, u32[]{:S(2)}) collective-permute-start(bf16[256,2,256]{2,0,1:T(8,128)(2,1)S(1)} %get-tuple-element.356), channel_id=1, source_target_pairs={{0,2},{2,4},{4,6},{6,8},{8,10},{10,12},{12,14},{14,16},{16,18},{18... | collective-permute-start | bytes 786440 | tf_op jit(solution)/shard_map/while/body/eval_jaxpr/ppermute | solution.py:22
  235.8 8.5 %collective-permute-start = (bf16[256,2,256]{2,0,1:T(8,128)(2,1)}, bf16[256,2,256]{2,0,1:T(8,128)(2,1)S(1)}, u32[]{:S(2)}, u32[]{:S(2)}) collective-permute-start(bf16[256,2,256]{2,0,1:T(8,128)(2,1)} %get-tuple-element.355), channel_id=1, source_target_pairs={{0,2},{2,4},{4,6},{6,8},{8,10},{10,12},{12,14},{14,16},{16,18},{18... | collective-permute-start | bytes 786440 | tf_op jit(solution)/shard_map/while/body/eval_jaxpr/ppermute | solution.py:22
  240.3 7.1 %collective-permute-start.1 = (bf16[256,2,256]{2,0,1:T(8,128)(2,1)S(1)}, bf16[256,2,256]{2,0,1:T(8,128)(2,1)S(1)}, u32[]{:S(2)}, u32[]{:S(2)}) collective-permute-start(bf16[256,2,256]{2,0,1:T(8,128)(2,1)S(1)} %get-tuple-element.356), channel_id=1, source_target_pairs={{0,2},{2,4},{4,6},{6,8},{8,10},{10,12},{12,14},{14,16},{16,18},{18... | collective-permute-start | bytes 786440 | tf_op jit(solution)/shard_map/while/body/eval_jaxpr/ppermute | solution.py:22
  248.0 8.5 %collective-permute-start = (bf16[256,2,256]{2,0,1:T(8,128)(2,1)}, bf16[256,2,256]{2,0,1:T(8,128)(2,1)S(1)}, u32[]{:S(2)}, u32[]{:S(2)}) collective-permute-start(bf16[256,2,256]{2,0,1:T(8,128)(2,1)} %get-tuple-element.355), channel_id=1, source_target_pairs={{0,2},{2,4},{4,6},{6,8},{8,10},{10,12},{12,14},{14,16},{16,18},{18... | collective-permute-start | bytes 786440 | tf_op jit(solution)/shard_map/while/body/eval_jaxpr/ppermute | solution.py:22
  252.5 7.1 %collective-permute-start.1 = (bf16[256,2,256]{2,0,1:T(8,128)(2,1)S(1)}, bf16[256,2,256]{2,0,1:T(8,128)(2,1)S(1)}, u32[]{:S(2)}, u32[]{:S(2)}) collective-permute-start(bf16[256,2,256]{2,0,1:T(8,128)(2,1)S(1)} %get-tuple-element.356), channel_id=1, source_target_pairs={{0,2},{2,4},{4,6},{6,8},{8,10},{10,12},{12,14},{14,16},{16,18},{18... | collective-permute-start | bytes 786440 | tf_op jit(solution)/shard_map/while/body/eval_jaxpr/ppermute | solution.py:22
  260.1 8.5 %collective-permute-start = (bf16[256,2,256]{2,0,1:T(8,128)(2,1)}, bf16[256,2,256]{2,0,1:T(8,128)(2,1)S(1)}, u32[]{:S(2)}, u32[]{:S(2)}) collective-permute-start(bf16[256,2,256]{2,0,1:T(8,128)(2,1)} %get-tuple-element.355), channel_id=1, source_target_pairs={{0,2},{2,4},{4,6},{6,8},{8,10},{10,12},{12,14},{14,16},{16,18},{18... | collective-permute-start | bytes 786440 | tf_op jit(solution)/shard_map/while/body/eval_jaxpr/ppermute | solution.py:22
  264.6 7.1 %collective-permute-start.1 = (bf16[256,2,256]{2,0,1:T(8,128)(2,1)S(1)}, bf16[256,2,256]{2,0,1:T(8,128)(2,1)S(1)}, u32[]{:S(2)}, u32[]{:S(2)}) collective-permute-start(bf16[256,2,256]{2,0,1:T(8,128)(2,1)S(1)} %get-tuple-element.356), channel_id=1, source_target_pairs={{0,2},{2,4},{4,6},{6,8},{8,10},{10,12},{12,14},{14,16},{16,18},{18... | collective-permute-start | bytes 786440 | tf_op jit(solution)/shard_map/while/body/eval_jaxpr/ppermute | solution.py:22
  272.3 8.5 %collective-permute-start = (bf16[256,2,256]{2,0,1:T(8,128)(2,1)}, bf16[256,2,256]{2,0,1:T(8,128)(2,1)S(1)}, u32[]{:S(2)}, u32[]{:S(2)}) collective-permute-start(bf16[256,2,256]{2,0,1:T(8,128)(2,1)} %get-tuple-element.355), channel_id=1, source_target_pairs={{0,2},{2,4},{4,6},{6,8},{8,10},{10,12},{12,14},{14,16},{16,18},{18... | collective-permute-start | bytes 786440 | tf_op jit(solution)/shard_map/while/body/eval_jaxpr/ppermute | solution.py:22
  276.7 7.1 %collective-permute-start.1 = (bf16[256,2,256]{2,0,1:T(8,128)(2,1)S(1)}, bf16[256,2,256]{2,0,1:T(8,128)(2,1)S(1)}, u32[]{:S(2)}, u32[]{:S(2)}) collective-permute-start(bf16[256,2,256]{2,0,1:T(8,128)(2,1)S(1)} %get-tuple-element.356), channel_id=1, source_target_pairs={{0,2},{2,4},{4,6},{6,8},{8,10},{10,12},{12,14},{14,16},{16,18},{18... | collective-permute-start | bytes 786440 | tf_op jit(solution)/shard_map/while/body/eval_jaxpr/ppermute | solution.py:22
  284.4 8.5 %collective-permute-start = (bf16[256,2,256]{2,0,1:T(8,128)(2,1)}, bf16[256,2,256]{2,0,1:T(8,128)(2,1)S(1)}, u32[]{:S(2)}, u32[]{:S(2)}) collective-permute-start(bf16[256,2,256]{2,0,1:T(8,128)(2,1)} %get-tuple-element.355), channel_id=1, source_target_pairs={{0,2},{2,4},{4,6},{6,8},{8,10},{10,12},{12,14},{14,16},{16,18},{18... | collective-permute-start | bytes 786440 | tf_op jit(solution)/shard_map/while/body/eval_jaxpr/ppermute | solution.py:22
  288.9 7.1 %collective-permute-start.1 = (bf16[256,2,256]{2,0,1:T(8,128)(2,1)S(1)}, bf16[256,2,256]{2,0,1:T(8,128)(2,1)S(1)}, u32[]{:S(2)}, u32[]{:S(2)}) collective-permute-start(bf16[256,2,256]{2,0,1:T(8,128)(2,1)S(1)} %get-tuple-element.356), channel_id=1, source_target_pairs={{0,2},{2,4},{4,6},{6,8},{8,10},{10,12},{12,14},{14,16},{16,18},{18... | collective-permute-start | bytes 786440 | tf_op jit(solution)/shard_map/while/body/eval_jaxpr/ppermute | solution.py:22
  (8 other events, 186.1 us)
Sparse Core Ops, SparseCore 0:
  9.6 83.3 all-gather.2
  95.3 56.9 all-gather.4
where the time goes:
time: 315 us; the launch traced here: 309 us
  starting transfers between devices  121 us (38%)
  waiting for transfers between devices  94 us (30%)
  matrix products  40.8 us (13%)
  local copies, waits for them, and re-layouts  15.9 us (5%)
  between operations  13.6 us (4%)
  other arithmetic  12 us (4%)
  blocking collectives  10.7 us (3%)
    ppermute x30, starting transfers between devices, from_behind(): return lax.ppermute(block, axis, route)  121 us
    all_gather x1, waiting for transfers between devices, per_device(): lax.all_gather(w_qkv, 'seq', axis=0, tiled=True)  69.1 us
    dot_general x16, matrix products, attend(): jnp.einsum('qhgd,khd->qhgk', queries, key_block, preferred_element_type=j...  24.1 us
    ppermute x30, waiting for transfers between devices, from_behind(): return lax.ppermute(block, axis, route)  23.4 us
    while x30, local copies, waits for them, and re-layouts  10.8 us
    pmin x1, blocking collectives, per_device(): first_pos = lax.pmin(local_first, 'seq')  10.7 us
    dot_general x16, matrix products, attend(): jnp.einsum('qhgk,khd->qhgd', weights.astype(jnp.bfloat16), value_block, p...  7.64 us
  transfers between devices with their start and end apart: 32, of which 19 were waited for; matrix products, arithmetic and copies ran while one was open for 20% of the time, Pallas kernels for 0%

commit v1 on v0

v1 whole, which is shorter than its diff:
```python
import math

import jax
import jax.numpy as jnp
from jax import lax
from jax.sharding import PartitionSpec as P

Q_HEADS = 4
KV_HEADS = 2
HEAD = 256
WINDOW = 4096
DOCS = 16


EPS = 1e-06
CAP = 50.0


def from_behind(block, axis, distance):
    devices = range(lax.axis_size(axis))
    route = [(i - distance, i) for i in devices if i - distance in devices]
    return lax.ppermute(block, axis, route)


def rms_scale(values, gain):
    return values * lax.rsqrt(jnp.mean(values * values, axis=-1, keepdims=True) + EPS) * gain


def rotary(values, positions, leading):
    head_size = values.shape[-1]
    half_dim = head_size // 2
    inverse = 1.0 / 10000.0 ** (jnp.arange(half_dim, dtype=jnp.float32) * 2.0 / head_size)
    angles = positions.astype(jnp.float32)[:, None] * inverse[None, :]
    shape = (
        (1,) * leading + (positions.shape[0],) + (1,) * (values.ndim - 2 - leading) + (half_dim,)
    )
    cosine = jnp.cos(angles).reshape(shape)
    sine = jnp.sin(angles).reshape(shape)
    first_half = values[..., :half_dim]
    second_half = values[..., half_dim:]
    return jnp.concatenate(
        [first_half * cosine - second_half * sine, second_half * cosine + first_half * sine],
        axis=-1,
    )


def per_device(hidden_in, segment_ids, pre_gain, w_qkv, w_out, post_gain):
    tok_rows = hidden_in.shape[1]
    seq_count = lax.axis_size("seq")
    seq_index = lax.axis_index("seq")
    groups = Q_HEADS // KV_HEADS
    doc_most = min(WINDOW, seq_count * tok_rows // 8)
    hops = min(-(-(doc_most - 1) // tok_rows), seq_count - 1)
    positions = seq_index * tok_rows + jnp.arange(tok_rows, dtype=jnp.int32)
    own_ids = segment_ids[0]
    id_blocks = [from_behind(own_ids, "seq", d) for d in range(hops, 0, -1)] + [own_ids]
    widened = hidden_in[0].astype(jnp.float32)
    normed = rms_scale(widened, pre_gain).astype(jnp.bfloat16)
    projected = jnp.dot(
        normed,
        lax.all_gather(w_qkv, "seq", axis=0, tiled=True),
        preferred_element_type=jnp.float32,
    )
    queries = rotary(
        projected[:, : Q_HEADS * HEAD].reshape(tok_rows, KV_HEADS, groups, HEAD), positions, 0
    ).astype(jnp.bfloat16)
    key_rows = rotary(
        projected[:, Q_HEADS * HEAD : (Q_HEADS + KV_HEADS) * HEAD].reshape(
            tok_rows, KV_HEADS, HEAD
        ),
        positions,
        0,
    ).astype(jnp.bfloat16)
    value_rows = projected[:, (Q_HEADS + KV_HEADS) * HEAD :].astype(jnp.bfloat16)
    both = jnp.concatenate([key_rows.reshape(tok_rows, KV_HEADS * HEAD), value_rows], axis=1)
    blocks = [from_behind(both, "seq", d) for d in range(hops, 0, -1)] + [both]
    kv = jnp.concatenate(blocks, axis=0).reshape(-1, 2, KV_HEADS, HEAD)
    ids = jnp.concatenate(id_blocks, axis=0)
    key_pos = (seq_index - hops) * tok_rows + jnp.arange((hops + 1) * tok_rows, dtype=jnp.int32)
    allowed = (
        (key_pos[None, :] >= 0)
        & (key_pos[None, :] <= positions[:, None])
        & (positions[:, None] - key_pos[None, :] < WINDOW)
        & (ids[None, :] == own_ids[:, None])
    )
    scores = jnp.einsum(
        "qhgd,khd->hgqk", queries, kv[:, 0], preferred_element_type=jnp.float32
    ) * (1.0 / math.sqrt(HEAD))
    capped = CAP * jnp.tanh(scores / CAP)
    weights = jnp.where(allowed[None, None], jnp.exp(capped), 0.0)
    totals = jnp.sum(weights, axis=-1)
    mixed = jnp.einsum(
        "hgqk,khd->hgqd", weights.astype(jnp.bfloat16), kv[:, 1], preferred_element_type=jnp.float32
    )
    attended = (mixed / totals[..., None]).astype(jnp.bfloat16)
    attended = attended.transpose(2, 0, 1, 3).reshape(tok_rows, Q_HEADS * HEAD)
    branch = jnp.dot(
        attended,
        lax.all_gather(w_out, "seq", axis=0, tiled=True),
        preferred_element_type=jnp.float32,
    )
    return (widened + rms_scale(branch, post_gain)).astype(jnp.bfloat16)[None]


def solution(mesh):
    placed = (P("batch", "seq", None), P("batch", "seq"), P(), P("seq", None), P("seq", None), P())
    return jax.shard_map(
        per_device, mesh=mesh, in_specs=placed, out_specs=P("batch", "seq", None), check_vma=False
    )
```

time: 315 us -> 167 us (0.53); the launches traced: 309 us -> 167 us
  starting transfers between devices: 121 us -> 14.5 us
  matrix products: 40.8 us -> 12.8 us
  waiting for transfers between devices: 94 us -> 109 us
  blocking collectives: 10.7 us -> 0 us
  local copies, waits for them, and re-layouts: 15.9 us -> 6.48 us
    ppermute x30 -> x4, starting transfers between devices: 121 us -> 14.4 us  [from_behind(): return lax.ppermute(block, axis, route)]
    dot_general x34 -> x4, matrix products: 40.8 us -> 12.8 us  [the longest x1 5.25 us: per_device(): jnp.dot(normed, lax.all_gather(w_qkv, 'seq', axis=0, tiled=True), preferr...]
    all_gather x1, waiting for transfers between devices: 0.02 us -> 23.1 us  [per_device(): lax.all_gather(w_out, 'seq', axis=0, tiled=True)]
    ppermute x30 -> x4, waiting for transfers between devices: 23.4 us -> 11.1 us  [from_behind(): return lax.ppermute(block, axis, route)]
    while x31 -> x0, local copies, waits for them, and re-layouts: 11.1 us -> none
    pmin x1 -> x0, blocking collectives: 10.7 us -> none  [per_device(): first_pos = lax.pmin(local_first, 'seq')]
    all_gather x1, waiting for transfers between devices: 69.1 us -> 73 us  [per_device(): lax.all_gather(w_qkv, 'seq', axis=0, tiled=True)]
  transfers between devices with their start and end apart: 32 -> 6, of which waited for: 19 -> 4; matrix products, arithmetic and copies ran while one was open for 20% -> 15% of each run, Pallas kernels for 0% -> 0%
where the time goes in v1:
time: 167 us
  waiting for transfers between devices  109 us (65%)
  starting transfers between devices  14.5 us (9%)
  between operations  13.7 us (8%)
  matrix products  12.8 us (8%)
  other arithmetic  10.6 us (6%)
  local copies, waits for them, and re-layouts  6.48 us (4%)
    all_gather x1, waiting for transfers between devices, per_device(): lax.all_gather(w_qkv, 'seq', axis=0, tiled=True)  73 us
    all_gather x1, waiting for transfers between devices, per_device(): lax.all_gather(w_out, 'seq', axis=0, tiled=True)  23.1 us
    ppermute x4, starting transfers between devices, from_behind(): return lax.ppermute(block, axis, route)  14.4 us
    ppermute x4, waiting for transfers between devices, from_behind(): return lax.ppermute(block, axis, route)  11.1 us
    dot_general x1, matrix products, per_device(): jnp.dot(normed, lax.all_gather(w_qkv, 'seq', axis=0, tiled=True), preferr...  5.25 us
    dot_general x1, matrix products, per_device(): jnp.dot(attended, lax.all_gather(w_out, 'seq', axis=0, tiled=True), prefe...  3.96 us
  transfers between devices with their start and end apart: 6, of which 4 were waited for; matrix products, arithmetic and copies ran while one was open for 15% of the time, Pallas kernels for 0%

profile of v1, /device:TPU:1, one launch (start us, length us, event | category | flops | bytes accessed | tf_op | source)
XLA Modules:
  0.0 166.6 jit_solution(11932889768963249122)
XLA Ops:
  6.5 0.7 all-gather.3.cloned.1.call-update
  7.3 0.0 all-gather.5.cloned.1.call-start
  7.3 0.7 all-gather.5.cloned.1.call-update
  8.0 4.5 %collective-permute-start.1 = (s32[256]{0:T(256)}, s32[256]{0:T(256)S(1)}, u32[]{:S(2)}, u32[]{:S(2)}) collective-permute-start(s32[256]{0:T(256)} %bitcast.51), channel_id=1, source_target_pairs={{0,2},{2,4},{4,6},{6,8},{8,10},{10,12},{12,14},{14,16},{16,18},{18... | collective-permute-start | bytes 3080 | tf_op jit(solution)/shard_map/ppermute | solution.py:22
  12.5 3.1 %collective-permute-start = (s32[256]{0:T(256)}, s32[256]{0:T(256)S(1)}, u32[]{:S(2)}, u32[]{:S(2)}) collective-permute-start(s32[256]{0:T(256)} %bitcast.52), channel_id=1, source_target_pairs={{0,4},{2,6},{4,8},{6,10},{8,12},{10,14},{12,16},{14,18},{16,20},{1... | collective-permute-start | bytes 3080 | tf_op jit(solution)/shard_map/ppermute | solution.py:22
  15.8 1.6 fusion
  17.3 1.3 multiply_cosine_fusion
  18.6 0.0 collective-permute-done.1
  18.6 0.0 collective-permute-done
  18.7 1.4 fusion.26
  20.0 73.0 %all-gather.3.cloned.1.call-done = bf16[2304,2048]{1,0:T(8,128)(2,1)} async-done(((bf16[144,2048]{1,0:T(8,128)(2,1)}), bf16[2304,2048]{1,0:T(8,128)(2,1)}) %all-gather.3.cloned.1.call-update) | async-done | bytes 9437200 | tf_op jit(solution)/shard_map/all_gather | solution.py:61
  93.0 5.2 %fusion.16 = f32[256,2048]{1,0:T(8,128)S(1)} fusion(bf16[2304,2048]{1,0:T(8,128)(2,1)} %all-gather.3.cloned.1.call-done, bf16[1,256,2304]{2,1,0:T(8,128)(2,1)S(1)} %copy-done, f32[2304]{0:T(1024)S(1)} %copy-done.10, f32[256]{0:T(256)S(1)} %add_rsqrt_fusion.1), kind=kOutput, calls=%fused_computation.19 | convolution fusion | flops 2418278400 | bytes 12724224 | tf_op jit(solution)/shard_map/dot_general | solution.py:59
  98.4 1.4 reshape.256
  99.8 1.4 subtract_convert_fusion.1
  101.2 0.3 pad_maximum_fusion.1
  101.6 0.9 pad_maximum_fusion
  102.4 2.4 %collective-permute-start.3 = (bf16[256,1024]{1,0:T(8,128)(2,1)}, bf16[256,1024]{1,0:T(8,128)(2,1)}, u32[]{:S(2)}, u32[]{:S(2)}) collective-permute-start(bf16[256,1024]{1,0:T(8,128)(2,1)} %pad_maximum_fusion), channel_id=1, source_target_pairs={{0,2},{2,4},{4,6},{6,8},{8,10},{10,12},{12,14},{14,16},{16,18},{18... | collective-permute-start | bytes 1572872 | tf_op jit(solution)/shard_map/ppermute | solution.py:22
  104.9 4.3 %collective-permute-start.2 = (bf16[256,1024]{1,0:T(8,128)(2,1)}, bf16[256,1024]{1,0:T(8,128)(2,1)}, u32[]{:S(2)}, u32[]{:S(2)}) collective-permute-start(bf16[256,1024]{1,0:T(8,128)(2,1)} %pad_maximum_fusion), channel_id=1, source_target_pairs={{0,4},{2,6},{4,8},{6,10},{8,12},{10,14},{12,16},{14,18},{16,20},{1... | collective-permute-start | bytes 1572872 | tf_op jit(solution)/shard_map/ppermute | solution.py:22
  109.2 0.9 reshape.258
  110.1 0.4 fusion.36
  110.5 0.9 subtract_convert_fusion
  111.4 2.7 %collective-permute-done.3 = bf16[256,1024]{1,0:T(8,128)(2,1)} collective-permute-done((bf16[256,1024]{1,0:T(8,128)(2,1)}, bf16[256,1024]{1,0:T(8,128)(2,1)}, u32[]{:S(2)}, u32[]{:S(2)}) %collective-permute-start.3) | collective-permute-done | bytes 524320 | tf_op jit(solution)/shard_map/ppermute | solution.py:22
  114.1 8.4 %collective-permute-done.2 = bf16[256,1024]{1,0:T(8,128)(2,1)} collective-permute-done((bf16[256,1024]{1,0:T(8,128)(2,1)}, bf16[256,1024]{1,0:T(8,128)(2,1)}, u32[]{:S(2)}, u32[]{:S(2)}) %collective-permute-start.2) | collective-permute-done | bytes 524320 | tf_op jit(solution)/shard_map/ppermute | solution.py:22
  122.5 1.3 maximum_maximum_fusion
  123.9 1.2 reshape.257
  125.1 2.0 %fusion.35 = (bf16[768,1,2,256]{3,2,1,0:T(2,128)(2,1)S(1)}, bf16[768,1,2,256]{3,2,1,0:T(2,128)(2,1)}) fusion(bf16[768,2,2,256]{3,2,1,0:T(2,128)(2,1)S(1)} %reshape.257), kind=kLoop, calls=%fused_computation.54 | loop fusion | bytes 3145728 | tf_op jit(solution)/shard_map/slice | solution.py:93
  127.0 0.6 copy.15
  127.6 2.4 %fusion.4 = (f32[2,2,256]{2,1,0:T(2,128)S(1)}, f32[2,768,256,2]{2,1,3,0:T(8,128)S(1)}) fusion(pred[256,768]{0,1:T(8,128)(4,1)} %fusion.26, bf16[256,2,2,128]{3,0,2,1:T(8,128)(2,1)} %get-tuple-element.8, bf16[256,2,2,128]{3,0,2,1:T(8,128)(2,1)S(1)} %copy-done.6, bf16[768,1,2,256]{3,2,1,0:T(2,128)(2,1)} %get-tuple-element.6), kind=kOutput, calls=%fused_computation.9 | convolution fusion | flops 406846464 | bytes 4657152 | tf_op jit(solution)/shard_map/qhgd,khd->hgqk/dot_general | solution.py:86
  130.1 1.2 divide_convert_fusion
  131.3 23.1 %all-gather.5.cloned.1.call-done = bf16[1024,2304]{1,0:T(8,128)(2,1)} async-done(((bf16[64,2304]{1,0:T(8,128)(2,1)}), bf16[1024,2304]{1,0:T(8,128)(2,1)}) %all-gather.5.cloned.1.call-update) | async-done | bytes 4718608 | tf_op jit(solution)/shard_map/all_gather | solution.py:99
  154.4 4.0 %multiply_reduce_fusion = (f32[256]{0:T(256)S(1)}, f32[256,2304]{1,0:T(8,128)S(1)}) fusion(bf16[256,1024]{0,1:T(8,128)(2,1)S(1)} %bitcast.49, bf16[1024,2304]{1,0:T(8,128)(2,1)} %all-gather.5.cloned.1.call-done), kind=kOutput, calls=%fused_computation.8 | convolution fusion | flops 1209138944 | bytes 7603200 | tf_op jit(solution)/shard_map/dot_general | solution.py:97
  158.3 1.4 fusion.15
  (36 shorter events, 0.2 us)
Async XLA Ops:
  6.5 12.1 %copy-start.9 = (s32[1,256]{1,0:T(1,128)S(1)}, s32[1,256]{1,0:T(1,128)}, u32[]{:S(2)}) copy-start(s32[1,256]{1,0:T(1,128)} %param.7) | copy-start | bytes 3076
  6.5 86.5 %copy-start = (bf16[1,256,2304]{2,1,0:T(8,128)(2,1)S(1)}, bf16[1,256,2304]{2,1,0:T(8,128)(2,1)}, u32[]{:S(2)}) copy-start(bf16[1,256,2304]{2,1,0:T(8,128)(2,1)} %param.6) | copy-start | bytes 3538948
  6.5 86.5 %copy-start.10 = (f32[2304]{0:T(1024)S(1)}, f32[2304]{0:T(1024)}, u32[]{:S(2)}) copy-start(f32[2304]{0:T(1024)} %param.8) | copy-start | bytes 27652
  6.5 86.5 %all-gather.3.cloned.1.call-start = ((), (), s32[]{:S(2)}) async-start(), calls=%async_computation | async-start | bytes 10027008 | tf_op jit(solution)/shard_map/all_gather | solution.py:61
  7.3 147.1 %all-gather.5.cloned.1.call-start = ((), (), s32[]{:S(2)}) async-start(), calls=%async_computation.1 | async-start | bytes 5013504 | tf_op jit(solution)/shard_map/all_gather | solution.py:99
  8.0 10.6 %collective-permute-start.1 = (s32[256]{0:T(256)}, s32[256]{0:T(256)S(1)}, u32[]{:S(2)}, u32[]{:S(2)}) collective-permute-start(s32[256]{0:T(256)} %bitcast.51), channel_id=1, source_target_pairs={{0,2},{2,4},{4,6},{6,8},{8,10},{10,12},{12,14},{14,16},{16,18},{18... | collective-permute-start | bytes 3080 | tf_op jit(solution)/shard_map/ppermute | solution.py:22
  12.5 6.1 %collective-permute-start = (s32[256]{0:T(256)}, s32[256]{0:T(256)S(1)}, u32[]{:S(2)}, u32[]{:S(2)}) collective-permute-start(s32[256]{0:T(256)} %bitcast.52), channel_id=1, source_target_pairs={{0,4},{2,6},{4,8},{6,10},{8,12},{10,14},{12,16},{14,18},{16,20},{1... | collective-permute-start | bytes 3080 | tf_op jit(solution)/shard_map/ppermute | solution.py:22
  98.3 1.5 copy-start.2
  98.3 1.5 copy-start.3
  99.8 9.4 %slice-start = ((f32[256,2048]{1,0:T(8,128)}), f32[256,1024]{1,0:T(8,128)S(1)}, s32[]{:S(2)}) async-start(f32[256,2048]{1,0:T(8,128)} %copy-done.2), calls=%async_computation.2 | async-start | bytes 2097152 | tf_op jit(solution)/shard_map/slice | solution.py:65
  102.4 8.0 %copy-start.4 = (f32[256,128]{1,0:T(8,128)S(1)}, f32[256,128]{1,0:T(8,128)}, u32[]{:S(2)}) copy-start(f32[256,128]{1,0:T(8,128)} %get-tuple-element.13) | copy-start | bytes 393220
  102.4 8.0 %copy-start.5 = (f32[256,128]{1,0:T(8,128)S(1)}, f32[256,128]{1,0:T(8,128)}, u32[]{:S(2)}) copy-start(f32[256,128]{1,0:T(8,128)} %get-tuple-element.14) | copy-start | bytes 393220
  102.4 11.7 %collective-permute-start.3 = (bf16[256,1024]{1,0:T(8,128)(2,1)}, bf16[256,1024]{1,0:T(8,128)(2,1)}, u32[]{:S(2)}, u32[]{:S(2)}) collective-permute-start(bf16[256,1024]{1,0:T(8,128)(2,1)} %pad_maximum_fusion), channel_id=1, source_target_pairs={{0,2},{2,4},{4,6},{6,8},{8,10},{10,12},{12,14},{14,16},{16,18},{18... | collective-permute-start | bytes 1572872 | tf_op jit(solution)/shard_map/ppermute | solution.py:22
  104.9 17.7 %collective-permute-start.2 = (bf16[256,1024]{1,0:T(8,128)(2,1)}, bf16[256,1024]{1,0:T(8,128)(2,1)}, u32[]{:S(2)}, u32[]{:S(2)}) collective-permute-start(bf16[256,1024]{1,0:T(8,128)(2,1)} %pad_maximum_fusion), channel_id=1, source_target_pairs={{0,4},{2,6},{4,8},{6,10},{8,12},{10,14},{12,16},{14,18},{16,20},{1... | collective-permute-start | bytes 1572872 | tf_op jit(solution)/shard_map/ppermute | solution.py:22
  125.1 2.5 %copy-start.6 = (bf16[256,2,2,128]{3,0,2,1:T(8,128)(2,1)S(1)}, bf16[256,2,2,128]{3,0,2,1:T(8,128)(2,1)}, u32[]{:S(2)}) copy-start(bf16[256,2,2,128]{3,0,2,1:T(8,128)(2,1)} %get-tuple-element.7) | copy-start | bytes 786436
  127.6 2.5 %copy-start.7 = (pred[256,768]{0,1:T(8,128)(4,1)S(1)}, pred[256,768]{0,1:T(8,128)(4,1)}, u32[]{:S(2)}) copy-start(pred[256,768]{0,1:T(8,128)(4,1)} %fusion.26) | copy-start | bytes 589828
  154.3 4.0 %copy-start.1 = (bf16[1,256,2304]{2,1,0:T(8,128)(2,1)S(1)}, bf16[1,256,2304]{2,1,0:T(8,128)(2,1)}, u32[]{:S(2)}) copy-start(bf16[1,256,2304]{2,1,0:T(8,128)(2,1)} %param.6) | copy-start | bytes 3538948
  154.4 4.0 %copy-start.8 = (f32[2304]{0:T(1024)S(1)}, f32[2304]{0:T(1024)}, u32[]{:S(2)}) copy-start(f32[2304]{0:T(1024)} %param.11) | copy-start | bytes 27652
Sparse Core Ops, SparseCore 0:
  9.6 83.3 all-gather.2
  95.3 58.9 all-gather.4

commit v2 on v1

--- a/solution.py
+++ b/solution.py
@@ -1,8 +1,11 @@
+import functools
 import math
 
 import jax
 import jax.numpy as jnp
 from jax import lax
+from jax.experimental import pallas as pl
+from jax.experimental.pallas import tpu as pltpu
 from jax.sharding import PartitionSpec as P
 
 Q_HEADS = 4
@@ -44,7 +47,7 @@
     )
 
 
-def per_device(hidden_in, segment_ids, pre_gain, w_qkv, w_out, post_gain):
+def plain_layer(hidden_in, segment_ids, pre_gain, w_qkv, w_out, post_gain):
     tok_rows = hidden_in.shape[1]
     seq_count = lax.axis_size("seq")
     seq_index = lax.axis_index("seq")
@@ -102,6 +105,354 @@
     return (widened + rms_scale(branch, post_gain)).astype(jnp.bfloat16)[None]
 
 
+class Gather:
+    def __init__(self, place, own_ref, full_ref, piece, send_sems, recv_sems):
+        self.place, self.own_ref, self.full_ref = place, own_ref, full_ref
+        self.piece, self.send_sems, self.recv_sems = piece, send_sems, recv_sems
+        self.steps = place["chips"] - 1
+        self.started = []
+
+    def slot(self, kind, hop, unit):
+        return (kind * self.steps + hop - 1) * 2 + unit
+
+    def spot(self, kind, hop, core, unit):
+        place = self.place
+        shift = -hop if kind == 0 else hop
+        third = (1, 2 * place["x"], 2 - 2 * place["x"])[kind]
+        device = place["chip_at"](place["ring"] + shift) * 2 + core
+        return self.piece(self.full_ref, device, third, unit)
+
+    def copy(self, source, target, slot, device):
+        return pltpu.make_async_remote_copy(
+            src_ref=source,
+            dst_ref=target,
+            send_sem=self.send_sems.at[slot],
+            recv_sem=self.recv_sems.at[slot],
+            device_id=device,
+            device_id_type=pl.DeviceIdType.MESH,
+        )
+
+    def send(self, source, target, slot, device):
+        moving = self.copy(source, target, slot, device)
+        moving.start()
+        self.started.append(moving)
+
+    def arrived(self, spot, slot):
+        self.copy(spot, spot, slot, self.place["sibling"]).wait_recv()
+
+    def first_hop(self):
+        place = self.place
+        for unit in range(2):
+            for kind, target in ((0, place["up"]), (1, place["down"])):
+                third = (1, 2 * place["x"])[kind]
+                self.send(
+                    self.piece(self.own_ref, 0, third, unit),
+                    self.piece(self.full_ref, place["seq"], third, unit),
+                    self.slot(kind, 1, unit),
+                    target,
+                )
+
+    def share_own(self):
+        rows = self.own_ref.shape[0]
+        mine = self.full_ref.at[pl.ds(pl.multiple_of(self.place["seq"] * rows, 16), rows), :]
+        self.send(self.own_ref, mine, 12 * self.steps, self.place["sibling"])
+
+    def relay(self, kind, hop, unit):
+        spot = self.spot(kind, hop, self.place["core"], unit)
+        self.send(spot, spot, self.slot(kind + 3, hop, unit), self.place["sibling"])
+
+    def take_x(self, hop):
+        for unit in range(2):
+            self.arrived(self.spot(2, hop, self.place["core"], unit), self.slot(2, hop, unit))
+            self.relay(2, hop, unit)
+
+    def step(self, hop):
+        place = self.place
+        for unit in range(2):
+            for kind, target in ((0, place["up"]), (1, place["down"])):
+                spot = self.spot(kind, hop, place["core"], unit)
+                self.arrived(spot, self.slot(kind, hop, unit))
+                if hop < self.steps:
+                    self.send(spot, spot, self.slot(kind, hop + 1, unit), target)
+                if kind == 1:
+                    self.send(spot, spot, self.slot(2, hop, unit), place["across"])
+                self.relay(kind, hop, unit)
+        if hop > 1:
+            self.take_x(hop - 1)
+
+    def finish(self):
+        self.take_x(self.steps)
+        other = 1 - self.place["core"]
+        for hop in range(1, self.steps + 1):
+            for kind in range(3):
+                for unit in range(2):
+                    self.arrived(self.spot(kind, hop, other, unit), self.slot(kind + 3, hop, unit))
+        rows = self.own_ref.shape[0]
+        start = (self.place["seq"] + 1 - 2 * self.place["core"]) * rows
+        theirs = self.full_ref.at[pl.ds(pl.multiple_of(start, 16), rows), :]
+        self.arrived(theirs, 12 * self.steps)
+
+    def drain(self):
+        for moving in self.started:
+            moving.wait_send()
+
+
+def make_piece(rows, width, by_rows):
+    def piece(ref, device, third, unit):
+        if by_rows:
+            part, columns = rows // 3, width // 2
+            return ref.at[
+                pl.ds(pl.multiple_of(device * rows + third * part, 16), part),
+                pl.ds(unit * columns, columns),
+            ]
+        columns = width // 6
+        return ref.at[
+            pl.ds(pl.multiple_of(device * rows, 16), rows),
+            pl.ds(pl.multiple_of(third * 2 * columns + unit * columns, 128), columns),
+        ]
+
+    return piece
+
+
+def layer_kernel(
+    chips, hid, ids_row, ids_col, cos, sin, pre, w_qkv, w_out, post, out,
+    wq, wo, nrm, qry, kv, kv1, kv2, id1, id2, acc, tot, att, branch,
+    q_send, q_recv, o_send, o_recv, s_send, s_recv, local_sem,
+):
+    seq, x = lax.axis_index("seq"), lax.axis_index("batch")
+    chip, core = seq // 2, seq % 2
+    half = chips // 2
+    layer, side = chip // 2, chip % 2
+    ring = (1 - side) * layer + side * (chips - 1 - layer)
+
+    def chip_at(position):
+        position = (position + chips) % chips
+        far = position // half
+        return (1 - far) * 2 * position + far * (2 * (chips - 1 - position) + 1)
+
+    def at(device_chip, device_core, batch):
+        return {"seq": device_chip * 2 + device_core, "batch": batch}
+
+    place = dict(
+        chips=chips, seq=seq, x=x, core=core, ring=ring, chip_at=chip_at,
+        sibling=at(chip, 1 - core, x), across=at(chip, core, 1 - x),
+        up=at(chip_at(ring + 1), core, x), down=at(chip_at(ring - 1), core, x),
+    )
+    after = at((chip + 1) % chips, core, x)
+    before = at((chip + chips - 1) % chips, core, x)
+    met = [place["sibling"], place["across"], place["up"], place["down"], after, before]
+    barrier = pltpu.get_barrier_semaphore()
+    for other in met:
+        pl.semaphore_signal(barrier, 1, device_id=other, device_id_type=pl.DeviceIdType.MESH)
+    pl.semaphore_wait(barrier, len(met))
+
+    gather_q = Gather(place, w_qkv, wq, make_piece(*w_qkv.shape, True), q_send, q_recv)
+    gather_o = Gather(place, w_out, wo, make_piece(*w_out.shape, False), o_send, o_recv)
+    gather_q.first_hop()
+    gather_q.share_own()
+    gather_o.share_own()
+    own_copies = []
+    for index, (source, full) in enumerate(((w_qkv, wq), (w_out, wo))):
+        rows = source.shape[0]
+        mine = full.at[pl.ds(pl.multiple_of(seq * rows, 16), rows), :]
+        own_copies.append(pltpu.make_async_copy(source, mine, local_sem.at[index]))
+        own_copies[-1].start()
+
+    def small(source, target, slot, device):
+        return pltpu.make_async_remote_copy(
+            src_ref=source, dst_ref=target, send_sem=s_send.at[slot], recv_sem=s_recv.at[slot],
+            device_id=device, device_id_type=pl.DeviceIdType.MESH,
+        )
+
+    ids_on = small(ids_row, id2, 0, after)
+    ids_on.start()
+
+    tokens, width = hid.shape
+    strip = 16
+
+    @pl.loop(0, tokens // strip)
+    def _(index):
+        rows = pl.ds(pl.multiple_of(index * strip, strip), strip)
+        nrm[rows, :] = rms_scale(hid[rows, :].astype(jnp.float32), pre[...]).astype(jnp.bfloat16)
+
+    ids_on.wait()
+
+    def pass_on(own, far, near, slot):
+        @pl.when(core == 0)
+        def _():
+            small(own, near, slot, place["sibling"]).start()
+
+        @pl.when(core == 1)
+        def _():
+            small(far, near, slot, place["sibling"]).start()
+
+    pass_on(ids_row, id2, id1, 1)
+
+    for hop in range(1, chips):
+        gather_q.step(hop)
+        if hop == chips - 1:
+            gather_o.first_hop()
+    gather_q.finish()
+    for moving in own_copies:
+        moving.wait()
+
+    def project(column):
+        return jnp.dot(
+            nrm[...], wq[:, column : column + HEAD], preferred_element_type=jnp.float32
+        )
+
+    def turned(values):
+        a, b = values[:, : HEAD // 2], values[:, HEAD // 2 :]
+        c, s = cos[...], sin[...]
+        return jnp.concatenate([a * c - b * s, b * c + a * s], axis=1).astype(jnp.bfloat16)
+
+    keys_at = Q_HEADS * HEAD
+    for head in range(KV_HEADS):
+        columns = slice(head * HEAD, (head + 1) * HEAD)
+        kv[:, columns] = turned(project(keys_at + head * HEAD))
+    for head in range(KV_HEADS, 2 * KV_HEADS):
+        columns = slice(head * HEAD, (head + 1) * HEAD)
+        kv[:, columns] = project(keys_at + head * HEAD).astype(jnp.bfloat16)
+    kv_on = small(kv, kv2, 2, after)
+    kv_on.start()
+    gather_o.step(1)
+    for head in range(Q_HEADS):
+        columns = slice(head * HEAD, (head + 1) * HEAD)
+        qry[:, columns] = turned(project(head * HEAD))
+        if head == 1:
+            gather_o.step(2)
+    gather_o.step(3)
+
+    def block(head, source, allowed, first):
+        group = head // (Q_HEADS // KV_HEADS)
+        columns = slice(head * HEAD, (head + 1) * HEAD)
+        keys = source[:, group * HEAD : (group + 1) * HEAD]
+        values = source[:, (KV_HEADS + group) * HEAD : (KV_HEADS + group + 1) * HEAD]
+        scores = lax.dot_general(
+            qry[:, columns], keys, (((1,), (1,)), ((), ())), preferred_element_type=jnp.float32
+        )
+        capped = CAP * jnp.tanh(scores * (1.0 / (math.sqrt(HEAD) * CAP)))
+        weights = jnp.where(allowed, jnp.exp(capped), 0.0)
+        total = jnp.sum(weights, axis=1, keepdims=True)
+        mixed = jnp.dot(weights.astype(jnp.bfloat16), values, preferred_element_type=jnp.float32)
+        if first:
+            acc[:, columns] = mixed
+            tot[:, head * 128 : (head + 1) * 128] = jnp.broadcast_to(total, (tokens, 128))
+        else:
+            acc[:, columns] += mixed
+            tot[:, head * 128 : (head + 1) * 128] += jnp.broadcast_to(total, (tokens, 128))
+
+    query_ids = ids_col[:, :1]
+    row = lax.broadcasted_iota(jnp.int32, (tokens, tokens), 0)
+    column = lax.broadcasted_iota(jnp.int32, (tokens, tokens), 1)
+    own_allowed = (column <= row) & (query_ids == ids_row[:1, :])
+    for head in range(Q_HEADS):
+        block(head, kv, own_allowed, True)
+        if head == 1:
+            gather_o.step(4)
+    gather_o.step(5)
+    small(ids_row, id1, 1, place["sibling"]).wait()
+    kv_on.wait()
+    pass_on(kv, kv2, kv1, 3)
+    far_allowed = (query_ids == id2[:1, :]) & (row + seq >= row + 2)
+    for head in range(Q_HEADS):
+        block(head, kv2, far_allowed, False)
+    gather_o.step(6)
+    small(kv, kv1, 3, place["sibling"]).wait()
+    near_allowed = (query_ids == id1[:1, :]) & (row + seq >= row + 1)
+    for head in range(Q_HEADS):
+        block(head, kv1, near_allowed, False)
+        columns = slice(head * HEAD, (head + 1) * HEAD)
+        att[:, columns] = (acc[:, columns] / tot[:, head * 128 : head * 128 + 1]).astype(
+            jnp.bfloat16
+        )
+    gather_o.step(7)
+    gather_o.finish()
+    for start in range(0, width, 256):
+        branch[:, start : start + 256] = jnp.dot(
+            att[...], wo[:, start : start + 256], preferred_element_type=jnp.float32
+        )
+
+    @pl.loop(0, tokens // strip)
+    def _(index):
+        rows = pl.ds(pl.multiple_of(index * strip, strip), strip)
+        scaled = rms_scale(branch[rows, :], post[...])
+        out[rows, :] = (hid[rows, :].astype(jnp.float32) + scaled).astype(jnp.bfloat16)
+
+    gather_q.drain()
+    gather_o.drain()
+
+
+def ring_layer(hidden_in, segment_ids, pre_gain, w_qkv, w_out, post_gain):
+    tokens, width = hidden_in.shape[1:]
+    seq_count = lax.axis_size("seq")
+    chips = seq_count // 2
+    positions = lax.axis_index("seq") * tokens + jnp.arange(tokens, dtype=jnp.int32)
+    inverse = 1.0 / 10000.0 ** (jnp.arange(HEAD // 2, dtype=jnp.float32) * 2.0 / HEAD)
+    angles = positions.astype(jnp.float32)[:, None] * inverse[None, :]
+    ids = segment_ids[0]
+    pieces = 12 * (chips - 1) + 1
+    bf16, f32 = jnp.bfloat16, jnp.float32
+    vmem, dma = pltpu.VMEM, pltpu.SemaphoreType.DMA
+    heads = Q_HEADS * HEAD
+    pairs = 2 * KV_HEADS * HEAD
+    result = pl.pallas_call(
+        functools.partial(layer_kernel, chips),
+        out_shape=jax.ShapeDtypeStruct((tokens, width), bf16),
+        in_specs=[pl.BlockSpec(memory_space=vmem)] * 9,
+        out_specs=pl.BlockSpec(memory_space=vmem),
+        scratch_shapes=[
+            vmem((width, w_qkv.shape[1]), bf16),
+            vmem((heads, width), bf16),
+            vmem((tokens, width), bf16),
+            vmem((tokens, heads), bf16),
+            vmem((tokens, pairs), bf16),
+            vmem((tokens, pairs), bf16),
+            vmem((tokens, pairs), bf16),
+            vmem((8, tokens), jnp.int32),
+            vmem((8, tokens), jnp.int32),
+            vmem((tokens, heads), f32),
+            vmem((tokens, Q_HEADS * 128), f32),
+            vmem((tokens, heads), bf16),
+            vmem((tokens, width), f32),
+            dma((pieces,)),
+            dma((pieces,)),
+            dma((pieces,)),
+            dma((pieces,)),
+            dma((4,)),
+            dma((4,)),
+            dma((2,)),
+        ],
+        compiler_params=pltpu.CompilerParams(
+            collective_id=0, has_side_effects=True, vmem_limit_bytes=58 * 1024 * 1024
+        ),
+    )(
+        hidden_in[0],
+        jnp.broadcast_to(ids[None, :], (8, tokens)),
+        jnp.broadcast_to(ids[:, None], (tokens, 128)),
+        jnp.cos(angles),
+        jnp.sin(angles),
+        pre_gain[None, :],
+        w_qkv,
+        w_out,
+        post_gain[None, :],
+    )
+    return result[None]
+
+
+def per_device(hidden_in, segment_ids, pre_gain, w_qkv, w_out, post_gain):
+    tokens = hidden_in.shape[1]
+    seq_count = lax.axis_size("seq")
+    doc_most = min(WINDOW, seq_count * tokens // 8)
+    whole_tiles = w_qkv.shape[0] % 48 == 0 and w_out.shape[0] % 16 == 0
+    two_hops = doc_most - 1 <= 2 * tokens and 3 * tokens <= WINDOW
+    if whole_tiles and two_hops and seq_count % 4 == 0 and lax.axis_size("batch") == 2:
+        layer = ring_layer
+    else:
+        layer = plain_layer
+    return layer(hidden_in, segment_ids, pre_gain, w_qkv, w_out, post_gain)
+
+
 def solution(mesh):
     placed = (P("batch", "seq", None), P("batch", "seq"), P(), P("seq", None), P("seq", None), P())
     return jax.shard_map(

time: 167 us -> 100 us (0.60)
  waiting for transfers between devices: 109 us -> 0 us
  Pallas kernels: 0 us -> 91.1 us
  starting transfers between devices: 14.5 us -> 0 us
  between operations: 13.7 us -> 0.01 us
  matrix products: 12.8 us -> 0 us
  other arithmetic: 10.6 us -> 1.26 us
    all_gather x2 -> x0, waiting for transfers between devices: 96.1 us -> none  [the longest x1 73 us: per_device(): lax.all_gather(w_qkv, 'seq', axis=0, tiled=True)]
    pallas_call x0 -> x1, Pallas kernels: none -> 91.1 us  [ring_layer(): pl.pallas_call(functools.partial(layer_kernel, chips), out_shape=jax.Shap...]
    ppermute x4 -> x0, starting transfers between devices: 14.4 us -> none  [from_behind(): return lax.ppermute(block, axis, route)]
    dot_general x4 -> x0, matrix products: 12.8 us -> none  [the longest x1 5.25 us: per_device(): jnp.dot(normed, lax.all_gather(w_qkv, 'seq', axis=0, tiled=True), preferr...]
    ppermute x4 -> x0, waiting for transfers between devices: 11.1 us -> none  [from_behind(): return lax.ppermute(block, axis, route)]
    broadcast_in_dim x0 -> x4, local copies, waits for them, and re-layouts: none -> 5.32 us  [the longest x1 1.43 us: ring_layer(): jnp.broadcast_to(ids[:, None], (tokens, 128))]
    reshape x3 -> x0, local copies, waits for them, and re-layouts: 3.44 us -> none  [the longest x1 1.37 us: per_device(): projected[:, Q_HEADS * HEAD:(Q_HEADS + KV_HEADS) * HEAD]]
    concatenate x4 -> x0, other arithmetic: 2.5 us -> none  [the longest x1 1.35 us: per_device(): kv = jnp.concatenate(blocks, axis=0).reshape(-1, 2, KV_HEADS, HEAD)]
  transfers between devices with their start and end apart: 6 -> 0, of which waited for: 4 -> 0; matrix products, arithmetic and copies ran while one was open for 15% -> 0% of each run, Pallas kernels for 0% -> 0%
where the time goes in v2:
time: 100 us
  Pallas kernels  91.1 us (91%)
  local copies, waits for them, and re-layouts  7.68 us (8%)
  other arithmetic  1.26 us (1%)
    pallas_call x1, Pallas kernels, ring_layer(): pl.pallas_call(functools.partial(layer_kernel, chips), out_shape=jax.Shap...  91.1 us
    unnamed x1, local copies, waits for them, and re-layouts  2.36 us

profile of v2, /device:TPU:1, one launch (start us, length us, event | category | flops | bytes accessed | tf_op | source)
XLA Modules:
  0.0 100.1 jit_solution(141841164501667355)
XLA Ops:
  0.0 1.3 %broadcast_in_dim.24.ids_row = s32[8,256]{1,0:T(8,128)} broadcast(s32[256]{0:T(256)} %bitcast.5), dimensions={1} | broadcast | bytes 9216 | tf_op jit(solution)/shard_map/broadcast_in_dim | solution.py:431
  1.3 1.3 %broadcast_in_dim.26.pre = f32[1,2304]{1,0:T(1,128)} reshape(f32[2304]{0:T(1024)} %param.8) | data formatting | bytes 18432 | tf_op jit(solution)/shard_map/broadcast_in_dim | solution.py:435
  2.6 1.3 %broadcast_in_dim.27.post = f32[1,2304]{1,0:T(1,128)} reshape(f32[2304]{0:T(1024)} %param.11) | data formatting | bytes 18432 | tf_op jit(solution)/shard_map/broadcast_in_dim | solution.py:438
  3.9 1.4 %broadcast_in_dim.25.ids_col = s32[256,128]{1,0:T(8,128)} broadcast(s32[256]{0:T(256)} %bitcast.6), dimensions={0} | broadcast | bytes 132096 | tf_op jit(solution)/shard_map/broadcast_in_dim | solution.py:432
  5.3 1.2 %multiply_sine_fusion = (f32[256,128]{1,0:T(8,128)}, f32[256,128]{1,0:T(8,128)}) fusion(f32[128]{0:T(128)S(1)} %negate_power_fusion, f32[256]{0:T(256)S(1)} %add_convert_fusion), kind=kLoop, calls=%fused_computation | loop fusion | flops 32768 | bytes 263680 | tf_op jit(solution)/shard_map/sin | solution.py:434
  6.6 91.1 %shard_map.64 = bf16[256,2304]{1,0:T(8,128)(2,1)} custom-call(bf16[256,2304]{1,0:T(8,128)(2,1)} %bitcast.4, s32[8,256]{1,0:T(8,128)} %broadcast_in_dim.24.ids_row, s32[256,128]{1,0:T(8,128)} %broadcast_in_dim.25.ids_col, f32[256,128]{1,0:T(8,128)} %get-tuple-element.6.cos, f32[256,128]{1,0:T(8,128)} %get-tuple-element.5.sin, ...), custom_call_target="tpu_custom_call" | custom-call | tf_op jit(solution)/shard_map/pallas_call | solution.py:399
  97.7 2.4 %copy.8 = bf16[1,256,2304]{2,1,0:T(8,128)(2,1)} copy(bf16[1,256,2304]{2,1,0:T(8,128)(2,1)} %bitcast.3) | data formatting | bytes 2359296
  (2 shorter events, 0.0 us)

commit v3 on v2

--- a/solution.py
+++ b/solution.py
@@ -142,7 +142,11 @@
 
     def first_hop(self):
         place = self.place
-        for unit in range(2):
+        for unit in (1, 0):
+            if unit == 0:
+                for moving in self.started[-2:]:
+                    moving.wait_send()
+                del self.started[-2:]
             for kind, target in ((0, place["up"]), (1, place["down"])):
                 third = (1, 2 * place["x"])[kind]
                 self.send(
@@ -161,14 +165,16 @@
         spot = self.spot(kind, hop, self.place["core"], unit)
         self.send(spot, spot, self.slot(kind + 3, hop, unit), self.place["sibling"])
 
-    def take_x(self, hop):
-        for unit in range(2):
+    def take_x(self, hop, units=(1, 0)):
+        for unit in units:
             self.arrived(self.spot(2, hop, self.place["core"], unit), self.slot(2, hop, unit))
             self.relay(2, hop, unit)
 
     def step(self, hop):
         place = self.place
-        for unit in range(2):
+        for unit in (1, 0):
+            if hop > 1:
+                self.take_x(hop - 1, (unit,))
             for kind, target in ((0, place["up"]), (1, place["down"])):
                 spot = self.spot(kind, hop, place["core"], unit)
                 self.arrived(spot, self.slot(kind, hop, unit))
@@ -177,16 +183,16 @@
                 if kind == 1:
                     self.send(spot, spot, self.slot(2, hop, unit), place["across"])
                 self.relay(kind, hop, unit)
-        if hop > 1:
-            self.take_x(hop - 1)
-
-    def finish(self):
-        self.take_x(self.steps)
+
+    def finish(self, units=(1, 0)):
+        self.take_x(self.steps, units)
         other = 1 - self.place["core"]
-        for hop in range(1, self.steps + 1):
-            for kind in range(3):
-                for unit in range(2):
+        for unit in units:
+            for hop in range(1, self.steps + 1):
+                for kind in range(3):
                     self.arrived(self.spot(kind, hop, other, unit), self.slot(kind + 3, hop, unit))
+        if 1 not in units:
+            return
         rows = self.own_ref.shape[0]
         start = (self.place["seq"] + 1 - 2 * self.place["core"]) * rows
         theirs = self.full_ref.at[pl.ds(pl.multiple_of(start, 16), rows), :]
@@ -248,9 +254,9 @@
 
     gather_q = Gather(place, w_qkv, wq, make_piece(*w_qkv.shape, True), q_send, q_recv)
     gather_o = Gather(place, w_out, wo, make_piece(*w_out.shape, False), o_send, o_recv)
-    gather_q.first_hop()
     gather_q.share_own()
     gather_o.share_own()
+    gather_q.first_hop()
     own_copies = []
     for index, (source, full) in enumerate(((w_qkv, wq), (w_out, wo))):
         rows = source.shape[0]
@@ -290,9 +296,11 @@
 
     for hop in range(1, chips):
         gather_q.step(hop)
-        if hop == chips - 1:
+        if hop == 1:
             gather_o.first_hop()
-    gather_q.finish()
+        elif hop > 1:
+            gather_o.step(hop - 1)
+    gather_q.finish((1,))
     for moving in own_copies:
         moving.wait()
 
@@ -315,13 +323,12 @@
         kv[:, columns] = project(keys_at + head * HEAD).astype(jnp.bfloat16)
     kv_on = small(kv, kv2, 2, after)
     kv_on.start()
-    gather_o.step(1)
+    for hop in range(chips - 1, chips):
+        gather_o.step(hop)
+    gather_q.finish((0,))
     for head in range(Q_HEADS):
         columns = slice(head * HEAD, (head + 1) * HEAD)
         qry[:, columns] = turned(project(head * HEAD))
-        if head == 1:
-            gather_o.step(2)
-    gather_o.step(3)
 
     def block(head, source, allowed, first):
         group = head // (Q_HEADS // KV_HEADS)
@@ -348,16 +355,12 @@
     own_allowed = (column <= row) & (query_ids == ids_row[:1, :])
     for head in range(Q_HEADS):
         block(head, kv, own_allowed, True)
-        if head == 1:
-            gather_o.step(4)
-    gather_o.step(5)
     small(ids_row, id1, 1, place["sibling"]).wait()
     kv_on.wait()
     pass_on(kv, kv2, kv1, 3)
     far_allowed = (query_ids == id2[:1, :]) & (row + seq >= row + 2)
     for head in range(Q_HEADS):
         block(head, kv2, far_allowed, False)
-    gather_o.step(6)
     small(kv, kv1, 3, place["sibling"]).wait()
     near_allowed = (query_ids == id1[:1, :]) & (row + seq >= row + 1)
     for head in range(Q_HEADS):
@@ -366,7 +369,6 @@
         att[:, columns] = (acc[:, columns] / tot[:, head * 128 : head * 128 + 1]).astype(
             jnp.bfloat16
         )
-    gather_o.step(7)
     gather_o.finish()
     for start in range(0, width, 256):
         branch[:, start : start + 256] = jnp.dot(
@@ -409,8 +411,8 @@
             vmem((tokens, pairs), bf16),
             vmem((tokens, pairs), bf16),
             vmem((tokens, pairs), bf16),
-            vmem((8, tokens), jnp.int32),
-            vmem((8, tokens), jnp.int32),
+            vmem((1, tokens), jnp.int32),
+            vmem((1, tokens), jnp.int32),
             vmem((tokens, heads), f32),
             vmem((tokens, Q_HEADS * 128), f32),
             vmem((tokens, heads), bf16),
@@ -428,14 +430,14 @@
         ),
     )(
         hidden_in[0],
-        jnp.broadcast_to(ids[None, :], (8, tokens)),
+        segment_ids,
         jnp.broadcast_to(ids[:, None], (tokens, 128)),
         jnp.cos(angles),
         jnp.sin(angles),
-        pre_gain[None, :],
+        pre_gain,
         w_qkv,
         w_out,
-        post_gain[None, :],
+        post_gain,
     )
     return result[None]
 
@@ -446,7 +448,7 @@
     doc_most = min(WINDOW, seq_count * tokens // 8)
     whole_tiles = w_qkv.shape[0] % 48 == 0 and w_out.shape[0] % 16 == 0
     two_hops = doc_most - 1 <= 2 * tokens and 3 * tokens <= WINDOW
-    if whole_tiles and two_hops and seq_count % 4 == 0 and lax.axis_size("batch") == 2:
+    if whole_tiles and two_hops and seq_count % 4 == 0 and seq_count > 12 and lax.axis_size("batch") == 2:
         layer = ring_layer
     else:
         layer = plain_layer

time: 100 us -> 88.5 us (0.89)
  Pallas kernels: 91.1 us -> 83.1 us
  local copies, waits for them, and re-layouts: 7.68 us -> 3.8 us
    pallas_call x1, Pallas kernels: 91.1 us -> 83.1 us  [ring_layer(): pl.pallas_call(functools.partial(layer_kernel, chips), out_shape=jax.Shap...]
    broadcast_in_dim x3 -> x0, local copies, waits for them, and re-layouts: 3.89 us -> none  [the longest x1 1.31 us: ring_layer(): post_gain[None, :]]
where the time goes in v3:
time: 88.5 us; the launch traced here: 88.2 us
  Pallas kernels  83.1 us (94%)
  local copies, waits for them, and re-layouts  3.8 us (4%)
  other arithmetic  1.26 us (1%)
    pallas_call x1, Pallas kernels, ring_layer(): pl.pallas_call(functools.partial(layer_kernel, chips), out_shape=jax.Shap...  83.1 us
    unnamed x1, local copies, waits for them, and re-layouts  2.36 us

profile of v3, /device:TPU:1, one launch (start us, length us, event | category | flops | bytes accessed | tf_op | source)
XLA Modules:
  0.0 88.2 jit_solution(9649584656294233656)
XLA Ops:
  0.0 1.4 %broadcast_in_dim.13.ids_col = s32[256,128]{1,0:T(8,128)} broadcast(s32[256]{0:T(256)} %bitcast.5), dimensions={0} | broadcast | bytes 132096 | tf_op jit(solution)/shard_map/broadcast_in_dim | solution.py:434
  1.5 1.2 %multiply_sine_fusion = (f32[256,128]{1,0:T(8,128)}, f32[256,128]{1,0:T(8,128)}) fusion(f32[128]{0:T(128)S(1)} %negate_power_fusion, f32[256]{0:T(256)S(1)} %add_convert_fusion), kind=kLoop, calls=%fused_computation | loop fusion | flops 32768 | bytes 263680 | tf_op jit(solution)/shard_map/sin | solution.py:436
  2.7 83.1 %shard_map.64 = bf16[256,2304]{1,0:T(8,128)(2,1)} custom-call(bf16[256,2304]{1,0:T(8,128)(2,1)} %bitcast.4, s32[1,256]{1,0:T(1,128)} %ids_row.1, s32[256,128]{1,0:T(8,128)} %broadcast_in_dim.13.ids_col, f32[256,128]{1,0:T(8,128)} %get-tuple-element.6.cos, f32[256,128]{1,0:T(8,128)} %get-tuple-element.5.sin, f32[2304]{0:T(1024)} %pre.1, ...), custom_call_target="tpu_custom_call" | custom-call | tf_op jit(solution)/shard_map/pallas_call | solution.py:401
  85.8 2.4 %copy.8 = bf16[1,256,2304]{2,1,0:T(8,128)(2,1)} copy(bf16[1,256,2304]{2,1,0:T(8,128)(2,1)} %bitcast.3) | data formatting | bytes 2359296
  (2 shorter events, 0.0 us)
